TPU v7x, 32 devices: a whole 2x2x4 slice. The times are simulated.
32 devices in a mesh: seq: 8 (over z, x), tp: 4 (over y, core).
Axes of the slice: x: 2, y: 2, z: 4, core: 2. Of those that a mesh axis runs over, the one named last changes fastest.
Arguments:
- prompt_keys: bfloat16 [8, 16384, 512], P(None, 'seq', 'tp'), may hold values from -6 to 16
- prompt_values: bfloat16 [8, 16384, 512], P(None, 'seq', 'tp'), may hold values from -6 to 6
- keep_mask: int32 [8, 128, 4], P(None, 'seq', 'tp'), may hold values from 0 to 1, as said below
- owner_sequence: int32 [8], replicated, may hold values from 0 to 7, each once
- step_queries: bfloat16 [8, 16, 4, 1024], P('seq', None, 'tp'), may hold values from -15 to 26
- new_keys: bfloat16 [8, 16, 512], P('seq', None, 'tp'), may hold values from -12 to 12
- new_values: bfloat16 [8, 16, 512], P('seq', None, 'tp'), may hold values from -6 to 6
Outputs:
- attended: bfloat16 [8, 16, 4, 1024], P('seq', None, 'tp')
Inputs may be any that keep to these rules, and one draw needn't show every extreme that they name: `keep_mask`: the last block of every sequence is kept for every head; every sequence and head keeps between 32 and 96 blocks.
All inputs are finite; a program needn't handle non-finite values.
Results may differ from a plain program's by a relative error of at most 0.009.
The roundings to bfloat16 on the way count: a program that leaves them out, or rounds other values in their place, can miss the bound.
Values may be sent and summed in bfloat16 or wider, within the bound.
No kernel may reach another device: no remote copies, remote signals or barrier semaphores. Data moves between devices by JAX's collectives and lax.ppermute only.
A program may use at most 128 MiB of HBM per device.

v0:
```python
import math

import jax
import jax.numpy as jnp
from jax import lax
from jax.sharding import PartitionSpec as P

KEEP = 96


floor_score = -1e30


def frequencies(half_width):
    position_index = jnp.arange(half_width).astype(jnp.float32)
    base_rate = jnp.exp(position_index * (-2.0 / (2 * half_width)) * math.log(500000.0))
    wavelength = 2.0 * math.pi / base_rate
    smooth = (8192.0 / wavelength - 1.0) / 3.0
    blended = (1.0 - smooth) * base_rate / 8.0 + smooth * base_rate
    return jnp.where(
        wavelength < 2048.0, base_rate, jnp.where(wavelength > 8192.0, base_rate / 8.0, blended)
    )


def rotate(vector, offset):
    half_width = vector.shape[-1] // 2
    angles = offset.astype(jnp.float32)[..., None] * frequencies(half_width)
    cosine = jnp.cos(angles)
    sine_part = jnp.sin(angles)
    lower_half = vector[..., :half_width]
    upper_half = vector[..., half_width:]
    return jnp.concatenate(
        [
            lower_half * cosine - upper_half * sine_part,
            upper_half * cosine + lower_half * sine_part,
        ],
        axis=-1,
    )


def select_blocks(mask_column, block_size):
    running = jnp.cumsum(mask_column)
    slot_index = jnp.arange(KEEP)
    chosen = jnp.sum((running[None, :] <= slot_index[:, None]).astype(jnp.int32), axis=1)
    chosen = jnp.minimum(chosen, mask_column.shape[0] - 1)
    live_slots = slot_index < running[-1]
    return (chosen, live_slots, (slot_index - chosen) * block_size)


def attend(query_rows, cached_keys, cached_values, live_tokens, fresh_keys, fresh_values, groups):
    score_scale = 1.0 / math.sqrt(query_rows.shape[-1])
    older = jnp.dot(query_rows, cached_keys.T, preferred_element_type=jnp.float32) * score_scale
    older = jnp.where(live_tokens[None, :], older, floor_score)
    new_scores = jnp.dot(query_rows, fresh_keys.T, preferred_element_type=jnp.float32) * score_scale
    row_step = jnp.arange(query_rows.shape[0]) // groups
    causal = row_step[:, None] >= jnp.arange(fresh_keys.shape[0])[None, :]
    new_scores = jnp.where(causal, new_scores, floor_score)
    highest = jnp.maximum(jnp.max(older, axis=1), jnp.max(new_scores, axis=1))
    older_weight = jnp.where(live_tokens[None, :], jnp.exp(older - highest[:, None]), 0.0)
    newer_weight = jnp.where(causal, jnp.exp(new_scores - highest[:, None]), 0.0)
    row_total = jnp.sum(older_weight, axis=1) + jnp.sum(newer_weight, axis=1)
    result = jnp.dot(
        (older_weight / row_total[:, None]).astype(jnp.bfloat16),
        cached_values,
        preferred_element_type=jnp.float32,
    )
    result = result + jnp.dot(
        (newer_weight / row_total[:, None]).astype(jnp.bfloat16),
        fresh_values,
        preferred_element_type=jnp.float32,
    )
    return result


def shards(
    prompt_keys, prompt_values, keep_mask, owner_sequence, step_queries, new_keys, new_values
):
    sequences, tokens_here, columns = prompt_keys.shape
    heads_here = keep_mask.shape[2]
    blocks_here = keep_mask.shape[1]
    head_width = columns // heads_here
    block_size = tokens_here // blocks_here
    owners = lax.axis_size("seq")
    step_count = step_queries.shape[1]
    groups = step_queries.shape[3] // head_width
    query_all = step_queries[0].reshape(step_count, heads_here, groups, head_width)
    fresh_all = new_keys[0].reshape(step_count, heads_here, head_width)
    fresh_vals = new_values[0].reshape(step_count, heads_here, head_width)
    step_index = jnp.arange(step_count)
    outgoing = (
        jnp.take(prompt_keys, owner_sequence, axis=0),
        jnp.take(prompt_values, owner_sequence, axis=0),
        jnp.take(keep_mask, owner_sequence, axis=0).astype(jnp.bfloat16),
    )
    got_keys, got_values, got_mask = (
        lax.all_to_all(outgoing[0], "seq", split_axis=0, concat_axis=0, tiled=True),
        lax.all_to_all(outgoing[1], "seq", split_axis=0, concat_axis=0, tiled=True),
        lax.all_to_all(outgoing[2], "seq", split_axis=0, concat_axis=0, tiled=True),
    )
    total_blocks = owners * blocks_here
    key_blocks = got_keys.reshape(total_blocks, block_size, heads_here, head_width)
    value_blocks = got_values.reshape(total_blocks, block_size, heads_here, head_width)
    mask_rows = (got_mask > 0.5).astype(jnp.int32).reshape(total_blocks, heads_here)
    counts = jnp.sum(mask_rows, axis=0)
    longest = lax.pmax(jnp.max(counts), "tp")
    positions = longest * block_size + step_index
    chosen, live_slots, offset = select_blocks(mask_rows[:, 0], block_size)
    picked = jnp.take(key_blocks[:, :, 0], chosen, axis=0)
    turned = (
        rotate(picked.astype(jnp.float32), offset[:, None])
        .astype(jnp.bfloat16)
        .reshape(KEEP * block_size, head_width)
    )
    kept_values = jnp.take(value_blocks[:, :, 0], chosen, axis=0).reshape(
        KEEP * block_size, head_width
    )
    live_tokens = jnp.repeat(live_slots, block_size)
    query_rows = (
        rotate(query_all[:, 0].astype(jnp.float32), positions[:, None])
        .astype(jnp.bfloat16)
        .reshape(step_count * groups, head_width)
    )
    fresh_turned = rotate(fresh_all[:, 0].astype(jnp.float32), positions).astype(jnp.bfloat16)
    result = attend(
        query_rows, turned, kept_values, live_tokens, fresh_turned, fresh_vals[:, 0], groups
    )
    outputs = [result.reshape(step_count, groups * head_width)]
    return jnp.stack(outputs, axis=1)[None].astype(jnp.bfloat16)


def solution(mesh):
    in_specs = (
        P(None, "seq", "tp"),
        P(None, "seq", "tp"),
        P(None, "seq", "tp"),
        P(),
        P("seq", None, "tp", None),
        P("seq", None, "tp"),
        P("seq", None, "tp"),
    )
    out_specs = P("seq", None, "tp", None)
    return jax.shard_map(shards, mesh=mesh, in_specs=in_specs, out_specs=out_specs, check_vma=False)
```

profile of v0, /device:TPU:0, one launch (start us, length us, event | category | flops | bytes accessed | tf_op | source)
XLA Modules:
  0.0 241.3 jit_solution(11264360466100786829)
XLA Ops:
  0.0 0.7 compare_select_fusion.1
  0.7 0.7 compare_and_fusion.1
  1.3 1.2 gather_fusion
  2.7 0.6 copy.12
  3.3 7.3 %all-to-all-start = ((bf16[8,16,1]{1,2,0:T(2,128)(2,1)}), bf16[8,16,1]{1,2,0:T(2,128)(2,1)S(1)}, u32[]{:S(2)}, u32[]{:S(2)}) async-start(bf16[8,16,1]{1,2,0:T(2,128)(2,1)} %copy.12), calls=%async_computation | async-start | bytes 8192 | tf_op jit(solution)/shard_map/all_to_all | solution.py:98
  10.5 5.2 %gather_fusion.1 = bf16[8,2048,128]{2,1,0:T(8,128)(2,1)} fusion(bf16[8,2048,128]{2,1,0:T(8,128)(2,1)} %param.11, s32[1024]{0:T(1024)S(1)} %pad_clamp_fusion.1), kind=kCustom, calls=%fused_computation.clone | custom fusion | bytes 8388640 | tf_op jit(solution)/shard_map/jit(_take)/gather | solution.py:91
  15.7 5.2 %gather_fusion.3 = bf16[8,2048,128]{2,1,0:T(8,128)(2,1)} fusion(bf16[8,2048,128]{2,1,0:T(8,128)(2,1)} %param.12, s32[1024]{0:T(1024)S(1)} %pad_clamp_fusion.1), kind=kCustom, calls=%fused_computation.2.clone | custom fusion | bytes 8388640 | tf_op jit(solution)/shard_map/jit(_take)/gather | solution.py:92
  21.0 7.6 %broadcast_select_fusion.1 = (bf16[8,2048,128]{2,1,0:T(8,128)(2,1)}, bf16[8,2048,128]{2,1,0:T(8,128)(2,1)}) fusion(bf16[8,2048,128]{2,1,0:T(8,128)(2,1)} %gather_fusion.1, pred[8]{0:T(512)(128)(4,1)S(1)} %compare_and_fusion.1, bf16[8,2048,128]{2,1,0:T(8,128)(2,1)} %gather_fusion.3), kind=kLoop, calls=%fused_computation.13 | loop fusion | flops 4194304 | bytes 16777224 | tf_op jit(solution)/shard_map/jit(_take)/select_n | solution.py:91
  28.6 98.9 %all_to_all.15 = bf16[8,2048,128]{2,1,0:T(8,128)(2,1)} all-to-all(bf16[8,2048,128]{2,1,0:T(8,128)(2,1)} %get-tuple-element.23), channel_id=1, replica_groups=mesh['seq'=8,'tp'=4] {'seq'}, dimensions={0} | all-to-all | bytes 8388608 | tf_op jit(solution)/shard_map/all_to_all | solution.py:96
  127.5 4.7 %all-to-all-start.2 = ((bf16[8,2048,128]{2,1,0:T(8,128)(2,1)}), bf16[8,2048,128]{2,1,0:T(8,128)(2,1)}, u32[]{:S(2)}, u32[]{:S(2)}) async-start(bf16[8,2048,128]{2,1,0:T(8,128)(2,1)} %get-tuple-element.24), calls=%async_computation.2 | async-start | bytes 8388608 | tf_op jit(solution)/shard_map/all_to_all | solution.py:97
  132.3 0.6 fusion.20
  133.0 5.6 %pmax.7 = s32[]{:T(128)} all-reduce(s32[]{:T(128)} %get-tuple-element.6), channel_id=1, replica_groups=mesh['seq'=8,'tp'=4] {'tp'}, use_global_device_ids=true, to_apply=%region_2.3 | all-reduce | flops 1 | bytes 8 | tf_op jit(solution)/shard_map/pmax | solution.py:105
  138.9 0.6 slice.39
  140.1 0.6 iota_compare_fusion.2
  141.3 0.3 multiply_cosine_fusion
  141.7 3.3 %gather_fusion.2 = bf16[96,128,128]{2,1,0:T(8,128)(2,1)S(1)} fusion(bf16[128,128,128]{2,1,0:T(8,128)(2,1)} %bitcast.30, s32[1024]{0:T(1024)S(1)} %pad_clamp_fusion), kind=kCustom, calls=%fused_computation.1.clone | custom fusion | bytes 6291840 | tf_op jit(solution)/shard_map/jit(_take)/gather | solution.py:108
  145.0 79.4 %all-to-all-done.2 = bf16[8,2048,128]{2,1,0:T(8,128)(2,1)} async-done(((bf16[8,2048,128]{2,1,0:T(8,128)(2,1)}), bf16[8,2048,128]{2,1,0:T(8,128)(2,1)}, u32[]{:S(2)}, u32[]{:S(2)}) %all-to-all-start.2) | async-done | bytes 4194336 | tf_op jit(solution)/shard_map/all_to_all | solution.py:97
  224.4 4.9 %gather_fusion.4 = bf16[96,128,128]{2,1,0:T(8,128)(2,1)} fusion(bf16[128,128,128]{2,1,0:T(8,128)(2,1)} %bitcast.11, s32[1024]{0:T(1024)S(1)} %pad_clamp_fusion), kind=kCustom, calls=%fused_computation.3.clone | custom fusion | bytes 6291840 | tf_op jit(solution)/shard_map/jit(_take)/gather | solution.py:114
  229.3 2.8 %select_convert_fusion = (f32[96,128,128]{2,1,0:T(8,128)S(1)}, bf16[96,128,128]{2,1,0:T(8,128)(2,1)S(1)}) fusion(bf16[96,128,128]{2,1,0:T(8,128)(2,1)S(1)} %gather_fusion.2, pred[96]{0:T(512)(128)(4,1)S(1)} %get-tuple-element.9, bf16[96,128,128]{2,1,0:T(8,128)(2,1)} %gather_fusion.4), kind=kLoop, calls=%fused_computation.17 | loop fusion | flops 4718592 | bytes 15728736 | tf_op jit(solution)/shard_map/convert_element_type | solution.py:110
  232.2 2.6 %subtract_convert_fusion = (bf16[96,128,64]{2,1,0:T(8,128)(2,1)S(1)}, bf16[96,128,64]{2,1,0:T(8,128)(2,1)S(1)}) fusion(f32[96,128,128]{2,1,0:T(8,128)S(1)} %get-tuple-element.21, f32[96,64]{1,0:T(8,128)S(1)} %get-tuple-element.20, f32[96,64]{1,0:T(8,128)S(1)} %get-tuple-element.19), kind=kLoop, calls=%fused_computation.10 | loop fusion | flops 6291456 | bytes 9486336 | tf_op jit(solution)/shard_map/convert.7
  234.8 2.5 %fusion.26 = (f32[128]{0:T(128)S(1)}, f32[128,12288]{1,0:T(8,128)S(1)}) fusion(bf16[12288,64]{1,0:T(8,128)(2,1)S(1)} %bitcast.32, bf16[12288,64]{1,0:T(8,128)(2,1)S(1)} %bitcast.31, bf16[128,64]{1,0:T(8,128)(2,1)S(1)} %get-tuple-element.14, bf16[128,64]{1,0:T(8,128)(2,1)S(1)} %get-tuple-element.13, pred[12288]{0:T(1024)(128)(4,1)S(1)} %broadcast_bitcast_fusion), kind=kOutput, calls=%fused_computation.76 | convolution fusion | flops 413728640 | bytes 9482752 | tf_op jit(solution)/shard_map/dot_general | solution.py:52
  237.3 1.4 fusion.1
  238.7 1.7 fusion.5
  240.6 0.6 convert_element_type.109
  (30 shorter events, 1.4 us)
Async XLA Ops:
  0.0 240.4 %copy-start = (bf16[1,16,128]{2,1,0:T(8,128)(2,1)S(1)}, bf16[1,16,128]{2,1,0:T(8,128)(2,1)}, u32[]{:S(2)}) copy-start(bf16[1,16,128]{2,1,0:T(8,128)(2,1)} %param.17) | copy-start | bytes 12292
  3.3 25.3 %all-to-all-start = ((bf16[8,16,1]{1,2,0:T(2,128)(2,1)}), bf16[8,16,1]{1,2,0:T(2,128)(2,1)S(1)}, u32[]{:S(2)}, u32[]{:S(2)}) async-start(bf16[8,16,1]{1,2,0:T(2,128)(2,1)} %copy.12), calls=%async_computation | async-start | bytes 8192 | tf_op jit(solution)/shard_map/all_to_all | solution.py:98
  127.5 4.7 %copy-start.1 = (bf16[1,16,1,1024]{3,1,2,0:T(8,128)(2,1)S(1)}, bf16[1,16,1,1024]{3,1,2,0:T(8,128)(2,1)}, u32[]{:S(2)}) copy-start(bf16[1,16,1,1024]{3,1,2,0:T(8,128)(2,1)} %param.15) | copy-start | bytes 98308
  127.5 4.8 %copy-start.2 = (bf16[1,16,128]{2,1,0:T(8,128)(2,1)S(1)}, bf16[1,16,128]{2,1,0:T(8,128)(2,1)}, u32[]{:S(2)}) copy-start(bf16[1,16,128]{2,1,0:T(8,128)(2,1)} %param.16) | copy-start | bytes 12292
  127.5 96.9 %all-to-all-start.2 = ((bf16[8,2048,128]{2,1,0:T(8,128)(2,1)}), bf16[8,2048,128]{2,1,0:T(8,128)(2,1)}, u32[]{:S(2)}, u32[]{:S(2)}) async-start(bf16[8,2048,128]{2,1,0:T(8,128)(2,1)} %get-tuple-element.24), calls=%async_computation.2 | async-start | bytes 8388608 | tf_op jit(solution)/shard_map/all_to_all | solution.py:97
where the time goes:
time: 242 us; the launch traced here: 241 us
  blocking collectives  105 us (43%)
  waiting for transfers between devices  79.4 us (33%)
  local copies, waits for them, and re-layouts  21.9 us (9%)
  other arithmetic  18.1 us (7%)
  starting transfers between devices  12 us (5%)
  matrix products  4.57 us (2%)
    all_to_all x1, blocking collectives, shards(): lax.all_to_all(outgoing[0], 'seq', split_axis=0, concat_axis=0, tiled=True)  98.9 us
    all_to_all x1, waiting for transfers between devices, shards(): lax.all_to_all(outgoing[1], 'seq', split_axis=0, concat_axis=0, tiled=True)  79.4 us
    select_n x1, other arithmetic, shards(): jnp.take(prompt_keys, owner_sequence, axis=0)  7.59 us
    all_to_all x1, starting transfers between devices, shards(): lax.all_to_all(outgoing[2], 'seq', split_axis=0, concat_axis=0, tiled=True)  7.28 us
    pmax x1, blocking collectives, shards(): longest = lax.pmax(jnp.max(counts), 'tp')  5.57 us
    gather x1, local copies, waits for them, and re-layouts, shards(): jnp.take(prompt_values, owner_sequence, axis=0)  5.25 us
    gather x1, local copies, waits for them, and re-layouts, shards(): jnp.take(prompt_keys, owner_sequence, axis=0)  5.2 us
    gather x1, local copies, waits for them, and re-layouts, shards(): jnp.take(value_blocks[:, :, 0], chosen, axis=0)  4.92 us
  transfers between devices with their start and end apart: 2, of which 1 were waited for; matrix products, arithmetic and copies ran while one was open for 10% of the time, Pallas kernels for 0%

commit v1 on v0

v1 whole, which is shorter than its diff:
```python
import functools
import math

import jax
import jax.numpy as jnp
from jax import lax
from jax.experimental import pallas as pl
from jax.experimental.pallas import tpu as pltpu
from jax.sharding import PartitionSpec as P

BF = jnp.bfloat16
F32 = jnp.float32
EXTRA = 8
floor_score = -1e30
HIGH = lax.Precision.HIGHEST


def frequencies(half_width):
    position_index = jnp.arange(half_width).astype(F32)
    base_rate = jnp.exp(position_index * (-2.0 / (2 * half_width)) * math.log(500000.0))
    wavelength = 2.0 * math.pi / base_rate
    smooth = (8192.0 / wavelength - 1.0) / 3.0
    blended = (1.0 - smooth) * base_rate / 8.0 + smooth * base_rate
    return jnp.where(
        wavelength < 2048.0, base_rate, jnp.where(wavelength > 8192.0, base_rate / 8.0, blended)
    )


def turn_table(positions, width):
    half = width // 2
    angles = positions.astype(F32)[:, None] * frequencies(half)
    cosine, sine = jnp.cos(angles), jnp.sin(angles)
    return jnp.concatenate([cosine, cosine, -sine, sine], axis=1)


def turned(x, cosine, sine):
    return x * cosine + pltpu.roll(x, x.shape[-1] // 2, x.ndim - 1) * sine


def pack_kernel(groups, width, query_ref, near_ref, far_ref, out_ref):
    steps = query_ref.shape[0]
    rows = groups * steps
    parts = [query_ref[:, g * width : (g + 1) * width] for g in range(groups)]
    near = near_ref[...]
    far = far_ref[...]
    counts = jnp.concatenate([near[0:2], far[0:2], near[4:8]], axis=0).astype(BF)
    for target in range(out_ref.shape[0]):
        for g in range(groups):
            out_ref[target, g * steps : (g + 1) * steps, :] = parts[g]
        out_ref[target, rows : rows + EXTRA, :] = counts


def attend_kernel(
    sizes,
    owner_ref,
    keep_ref,
    rank_ref,
    base_ref,
    table_ref,
    step_ref,
    got_ref,
    key_ref,
    value_ref,
    out_ref,
    own_ref,
    cos_k,
    sin_k,
    cos_q,
    sin_q,
    score_ref,
):
    owners, blocks, block, groups, steps, width, heads, chunk = sizes
    rows = groups * steps
    me = rank_ref[0]
    lanes = owners * blocks
    before = jnp.zeros((1, lanes), F32)
    total = jnp.zeros((heads, lanes), F32)
    for i in range(owners):
        piece = got_ref[i, rows : rows + EXTRA, :].astype(F32)
        total = total + piece[0:heads]
        before = before + jnp.where(i < me, piece[0:1], 0.0)
    longest = jnp.max(total, axis=0, keepdims=True)
    dropped = base_ref[0:1, :] - before
    entry = lax.broadcasted_iota(jnp.int32, (table_ref.shape[0], lanes), 0).astype(F32)
    pick_k = (entry == dropped).astype(F32)
    pick_q = (entry == longest).astype(F32)
    dims = (((0,), (0,)), ((), ()))
    for pick, cos_to, sin_to in ((pick_k, cos_k, sin_k), (pick_q, cos_q, sin_q)):
        found = lax.dot_general(
            pick, table_ref[...], dims, precision=HIGH, preferred_element_type=F32
        )
        cos_to[...] = found[:, 0:width]
        sin_to[...] = found[:, width:]
    step_cos, step_sin = step_ref[:, 0:width], step_ref[:, width:]
    factor = math.log2(math.e) / math.sqrt(width)
    lane = lax.broadcasted_iota(jnp.int32, (rows, width), 1)

    def query_turn(s):
        cos0 = cos_q[pl.ds(s * blocks, 1), :]
        sin0 = sin_q[pl.ds(s * blocks, 1), :]
        return cos0 * step_cos - sin0 * step_sin, sin0 * step_cos + cos0 * step_sin

    own_cos, own_sin = query_turn(owner_ref[me])
    own_ref[:, 0:width] = own_cos
    own_ref[:, width:] = own_sin

    @pl.loop(0, owners)
    def _(o):
        s = owner_ref[o]
        cos_now, sin_now = query_turn(s)
        query = got_ref[o, 0:rows, :].astype(F32).reshape(groups, steps, width)
        swapped = pltpu.roll(query.reshape(rows, width), width // 2, 1)
        query = query * cos_now[None] + swapped.reshape(groups, steps, width) * sin_now[None]
        query = query.reshape(rows, width).astype(BF)
        best = jnp.full((rows, width), floor_score, F32)
        per = chunk // block
        for c in range(blocks // per):
            keys = []
            for j in range(per):
                b = c * per + j
                cosine = cos_k[pl.ds(s * blocks + b, 1), :]
                sine = sin_k[pl.ds(s * blocks + b, 1), :]
                x = key_ref[s, b * block : (b + 1) * block, :].astype(F32)
                keys.append(turned(x, cosine, -sine).astype(BF))
            scores = lax.dot_general(
                query,
                jnp.concatenate(keys, axis=0),
                (((1,), (1,)), ((), ())),
                preferred_element_type=F32,
            )
            for j in range(per):
                b = c * per + j
                bias = jnp.where(keep_ref[s * blocks + b] > 0, 0.0, floor_score)
                piece = scores[:, j * block : (j + 1) * block] + bias
                score_ref[:, b * block : (b + 1) * block] = piece
                best = jnp.maximum(best, piece)
        shift = (jnp.max(best, axis=1, keepdims=True) * factor).astype(BF).astype(F32)
        sums = jnp.zeros((rows, block), F32)
        result = jnp.zeros((rows, width), F32)
        for c in range(blocks // per):
            weights = []
            for j in range(per):
                b = c * per + j
                w = jnp.exp2(score_ref[:, b * block : (b + 1) * block] * factor - shift)
                sums = sums + w
                weights.append(w.astype(BF))
            result = result + jnp.dot(
                jnp.concatenate(weights, axis=1),
                value_ref[s, c * chunk : (c + 1) * chunk, :],
                preferred_element_type=F32,
            )
        mass = jnp.sum(sums, axis=1, keepdims=True)
        high = mass.astype(BF).astype(F32)
        notes = jnp.where(lane == 0, shift, jnp.where(lane == 1, high, mass - high))
        out_ref[o, 0:rows, :] = result.astype(BF)
        out_ref[o, rows : rows + EXTRA, :] = notes.T[0:EXTRA].astype(BF)


def fresh_kernel(groups, width, query_ref, own_ref, key_ref, value_ref, out_ref, note_ref):
    steps = query_ref.shape[0]
    rows = groups * steps
    cosine, sine = own_ref[:, 0:width], own_ref[:, width:]
    query = jnp.concatenate(
        [
            turned(query_ref[:, g * width : (g + 1) * width].astype(F32), cosine, sine)
            for g in range(groups)
        ],
        axis=0,
    ).astype(BF)
    fresh = turned(key_ref[...].astype(F32), cosine, sine).astype(BF)
    scores = lax.dot_general(
        query, fresh, (((1,), (1,)), ((), ())), preferred_element_type=F32
    )
    factor = math.log2(math.e) / math.sqrt(width)
    step = lax.rem(lax.broadcasted_iota(jnp.int32, (rows, steps), 0), steps)
    other = lax.broadcasted_iota(jnp.int32, (rows, steps), 1)
    scores = jnp.where(other <= step, scores * factor, floor_score)
    shift = jnp.max(scores, axis=1, keepdims=True)
    weights = jnp.exp2(scores - shift)
    mass = jnp.sum(weights, axis=1, keepdims=True)
    out_ref[...] = jnp.dot(weights.astype(BF), value_ref[...], preferred_element_type=F32)
    lane = lax.broadcasted_iota(jnp.int32, (rows, width), 1)
    note_ref[...] = jnp.where(lane == 0, shift, mass).T[0:EXTRA]


def merge_kernel(groups, steps, got_ref, fresh_ref, note_ref, out_ref):
    owners = got_ref.shape[0]
    width = got_ref.shape[2]
    rows = groups * steps
    shifts = [note_ref[0:1, :]]
    masses = [note_ref[1:2, :]]
    for i in range(owners):
        piece = got_ref[i, rows : rows + EXTRA, :].astype(F32)
        shifts.append(piece[0:1])
        masses.append(piece[1:2] + piece[2:3])
    top = functools.reduce(jnp.maximum, shifts)
    scales = [jnp.exp2(x - top) for x in shifts]
    mass = sum(a * b for a, b in zip(scales, masses))
    scales = [x / mass for x in scales]
    columns = []
    for first in range(0, owners + 1, rows):
        some = scales[first : first + rows]
        pad = jnp.zeros((rows - len(some), rows), F32)
        columns.append(jnp.concatenate(some + [pad], axis=0).T)
    result = fresh_ref[...] * columns[0][:, 0:1]
    for i in range(owners):
        k = i + 1
        result = result + got_ref[i, 0:rows, :].astype(F32) * columns[k // rows][
            :, k % rows : k % rows + 1
        ]
    result = result.astype(BF)
    for g in range(groups):
        out_ref[:, g * width : (g + 1) * width] = result[g * steps : (g + 1) * steps, :]


VMEM = pl.BlockSpec(memory_space=pltpu.VMEM)
SMEM = pl.BlockSpec(memory_space=pltpu.SMEM)


def shards(
    prompt_keys, prompt_values, keep_mask, owner_sequence, step_queries, new_keys, new_values
):
    sequences, tokens_here, width = prompt_keys.shape
    blocks = keep_mask.shape[1]
    block = tokens_here // blocks
    owners = lax.axis_size("seq")
    heads = lax.axis_size("tp")
    rank = lax.axis_index("seq")
    steps = step_queries.shape[1]
    groups = step_queries.shape[3] // width
    rows = groups * steps
    lanes = sequences * blocks
    query = step_queries.reshape(steps, groups * width)
    fresh_keys = new_keys.reshape(steps, width)
    fresh_values = new_values.reshape(steps, width)

    mask = keep_mask.reshape(sequences, blocks)
    count = jnp.sum(mask, axis=1).astype(F32)
    slot = jnp.sum(
        jnp.where(jnp.arange(blocks)[None, :, None] > jnp.arange(blocks)[None, None, :],
                  mask[:, None, :], 0), axis=2)
    base = (rank * blocks + jnp.arange(blocks)[None, :] - slot).astype(F32).reshape(1, lanes)
    base = jnp.broadcast_to(base, (EXTRA, lanes))
    own = jnp.repeat(count, blocks).reshape(1, lanes)
    own = jnp.broadcast_to(own, (EXTRA, lanes))
    other = lax.ppermute(own, "tp", [(i, i ^ 1) for i in range(heads)])
    row = lax.broadcasted_iota(jnp.int32, (EXTRA, lanes), 0)
    near = jnp.where(row == 0, own, jnp.where(row == 1, other, 0.0))
    far = lax.ppermute(near, "tp", [(i, i ^ 2) for i in range(heads)])

    payload = pl.pallas_call(
        functools.partial(pack_kernel, groups, width),
        out_shape=jax.ShapeDtypeStruct((owners, rows + EXTRA, width), BF),
        in_specs=[VMEM] * 3,
        out_specs=VMEM,
        name="pack",
    )(query, near, far)
    got = lax.all_to_all(payload, "seq", split_axis=0, concat_axis=0, tiled=True)

    table = turn_table(jnp.arange(owners * blocks) * block, width)
    step_table = turn_table(jnp.arange(steps), width)
    sizes = (owners, blocks, block, groups, steps, width, heads, min(4, blocks) * block)
    partial, own_turn = pl.pallas_call(
        functools.partial(attend_kernel, sizes),
        out_shape=(
            jax.ShapeDtypeStruct((owners, rows + EXTRA, width), BF),
            jax.ShapeDtypeStruct((steps, 2 * width), F32),
        ),
        in_specs=[SMEM, SMEM, SMEM] + [VMEM] * 6,
        out_specs=(VMEM, VMEM),
        scratch_shapes=[
            pltpu.VMEM((lanes, width), F32),
            pltpu.VMEM((lanes, width), F32),
            pltpu.VMEM((lanes, width), F32),
            pltpu.VMEM((lanes, width), F32),
            pltpu.VMEM((rows, tokens_here), F32),
        ],
        compiler_params=pltpu.CompilerParams(vmem_limit_bytes=40 * 1024 * 1024),
        name="attend",
    )(
        owner_sequence,
        mask.reshape(lanes),
        rank.reshape(1).astype(jnp.int32),
        base,
        table,
        step_table,
        got,
        prompt_keys,
        prompt_values,
    )
    back = lax.all_to_all(partial, "seq", split_axis=0, concat_axis=0, tiled=True)
    fresh, notes = pl.pallas_call(
        functools.partial(fresh_kernel, groups, width),
        out_shape=(
            jax.ShapeDtypeStruct((rows, width), F32),
            jax.ShapeDtypeStruct((EXTRA, rows), F32),
        ),
        in_specs=[VMEM] * 4,
        out_specs=(VMEM, VMEM),
        cost_estimate=pl.CostEstimate(
            flops=4 * rows * steps * width, bytes_accessed=4 * rows * width, transcendentals=0
        ),
        name="fresh",
    )(query, own_turn, fresh_keys, fresh_values)
    merged = pl.pallas_call(
        functools.partial(merge_kernel, groups, steps),
        out_shape=jax.ShapeDtypeStruct((steps, groups * width), BF),
        in_specs=[VMEM] * 3,
        out_specs=VMEM,
        name="merge",
    )(back, fresh, notes)
    return merged.reshape(1, steps, 1, groups * width)


def solution(mesh):
    in_specs = (
        P(None, "seq", "tp"),
        P(None, "seq", "tp"),
        P(None, "seq", "tp"),
        P(),
        P("seq", None, "tp", None),
        P("seq", None, "tp"),
        P("seq", None, "tp"),
    )
    out_specs = P("seq", None, "tp", None)
    return jax.shard_map(shards, mesh=mesh, in_specs=in_specs, out_specs=out_specs, check_vma=False)
```

time: 242 us -> 55.4 us (0.23)
  blocking collectives: 105 us -> 0 us
  waiting for transfers between devices: 79.4 us -> 16.6 us
  other arithmetic: 18.1 us -> 3.22 us
  local copies, waits for them, and re-layouts: 21.9 us -> 7.76 us
  Pallas kernels: 0 us -> 14.1 us
  matrix products: 4.57 us -> 0 us
    all_to_all x1 -> x0, blocking collectives: 98.9 us -> none  [shards(): lax.all_to_all(outgoing[0], 'seq', split_axis=0, concat_axis=0, tiled=True)]
    all_to_all x2, waiting for transfers between devices: 79.4 us -> 15 us  [the longest x1 8.08 us: shards(): lax.all_to_all(payload, 'seq', split_axis=0, concat_axis=0, tiled=True)]
    gather x5 -> x0, local copies, waits for them, and re-layouts: 19.9 us -> none  [the longest x1 5.25 us: shards(): jnp.take(prompt_values, owner_sequence, axis=0)]
    pallas_call x0 -> x4, Pallas kernels: none -> 14.1 us  [the longest x1 8.77 us: shards(): pl.pallas_call(functools.partial(attend_kernel, sizes), out_shape=(jax.Sh...]
    select_n x3 -> x1, other arithmetic: 8.26 us -> 0.07 us  [shards(): near = jnp.where(row == 0, own, jnp.where(row == 1, other, 0.0))]
    unnamed x7 -> x15, local copies, waits for them, and re-layouts: 0.03 us -> 7.44 us
    pmax x1 -> x0, blocking collectives: 5.57 us -> none  [shards(): longest = lax.pmax(jnp.max(counts), 'tp')]
    dot_general x4 -> x0, matrix products: 4.57 us -> none  [the longest x1 2.5 us: attend(): jnp.dot(query_rows, cached_keys.T, preferred_element_type=jnp.float32)]
  transfers between devices with their start and end apart: 2 -> 4, of which waited for: 1 -> 3; matrix products, arithmetic and copies ran while one was open for 10% -> 3% of each run, Pallas kernels for 0% -> 3%
where the time goes in v1:
time: 55.4 us; the launch traced here: 54.8 us
  waiting for transfers between devices  16.6 us (30%)
  Pallas kernels  14.1 us (25%)
  starting transfers between devices  13 us (23%)
  local copies, waits for them, and re-layouts  7.76 us (14%)
  other arithmetic  3.22 us (6%)
    pallas_call x1, Pallas kernels, shards(): pl.pallas_call(functools.partial(attend_kernel, sizes), out_shape=(jax.Sh...  8.77 us
    all_to_all x1, waiting for transfers between devices, shards(): lax.all_to_all(payload, 'seq', split_axis=0, concat_axis=0, tiled=True)  8.08 us
    unnamed x15, local copies, waits for them, and re-layouts  7.44 us
    all_to_all x1, waiting for transfers between devices, shards(): lax.all_to_all(partial, 'seq', split_axis=0, concat_axis=0, tiled=True)  6.96 us
    all_to_all x1, starting transfers between devices, shards(): lax.all_to_all(payload, 'seq', split_axis=0, concat_axis=0, tiled=True)  6.31 us
    all_to_all x1, starting transfers between devices, shards(): lax.all_to_all(partial, 'seq', split_axis=0, concat_axis=0, tiled=True)  3.57 us
    ppermute x1, starting transfers between devices, shards(): far = lax.ppermute(near, 'tp', [(i, i ^ 2) for i in range(heads)])  2.57 us
    pallas_call x1, Pallas kernels, shards(): pl.pallas_call(functools.partial(merge_kernel, groups, steps), out_shape=...  2 us
  transfers between devices with their start and end apart: 4, of which 3 were waited for; matrix products, arithmetic and copies ran while one was open for 3% of the time, Pallas kernels for 3%

profile of v1, /device:TPU:0, one launch (start us, length us, event | category | flops | bytes accessed | tf_op | source)
XLA Modules:
  0.0 54.8 jit_solution(17171759084537740196)
XLA Ops:
  0.0 0.5 broadcast.118
  0.5 1.6 %fusion.2 = (s32[8]{0:T(128)S(1)}, s32[8,16]{1,0:T(8,128)S(1)}) fusion(s32[8,16,1]{1,2,0:T(1,128)} %param.9, s32[]{:T(128)} %broadcast.118), kind=kLoop, calls=%fused_computation.19 | loop fusion | flops 120 | bytes 1060 | tf_op jit(solution)/shard_map/reduce_sum | solution.py:238
  2.2 0.1 broadcast_in_dim.54
  2.2 0.5 collective-permute-start
  2.8 0.9 %select_reduce_fusion = s32[8,16]{1,0:T(8,128)S(1)} fusion(s32[8,16]{1,0:T(8,128)} %bitcast.9, pred[16,16]{1,0:T(8,128)(4,1)S(1)} %iota_compare_fusion), kind=kLoop, calls=%fused_computation.3 | loop fusion | flops 3968 | bytes 1280 | tf_op jit(solution)/shard_map/reduce_sum | solution.py:239
  3.7 0.1 multiply_cosine_fusion.1
  4.0 2.6 %collective-permute-start.1 = (f32[8,128]{1,0:T(8,128)S(1)}, f32[8,128]{1,0:T(8,128)S(1)}, u32[]{:S(2)}, u32[]{:S(2)}) collective-permute-start(f32[8,128]{1,0:T(8,128)S(1)} %select_select_fusion.near_ref), channel_id=1, source_target_pairs={{0,2},{1,3},{2,0},{3,1},{4,6},{5,7},{6,4},{7,5},{8,10},{9,11},{10,... | collective-permute-start | bytes 12296 | tf_op jit(solution)/shard_map/ppermute | solution.py:249
  6.5 1.6 %collective-permute-done.1.far_ref = f32[8,128]{1,0:T(8,128)S(1)} collective-permute-done((f32[8,128]{1,0:T(8,128)S(1)}, f32[8,128]{1,0:T(8,128)S(1)}, u32[]{:S(2)}, u32[]{:S(2)}) %collective-permute-start.1) | collective-permute-done | bytes 4128 | tf_op jit(solution)/shard_map/ppermute | solution.py:249
  8.1 0.6 %copy-done.6 = f32[8,128]{1,0:T(8,128)} copy-done((f32[8,128]{1,0:T(8,128)}, f32[8,128]{1,0:T(8,128)S(1)}, u32[]{:S(2)}) %copy-start.6) | copy-done | bytes 4120
  8.7 1.5 %pack.1 = bf16[8,136,128]{2,1,0:T(8,128)(2,1)} custom-call(bf16[16,1024]{1,0:T(8,128)(2,1)} %bitcast.7, f32[8,128]{1,0:T(8,128)} %copy-done.5, f32[8,128]{1,0:T(8,128)} %copy-done.6), custom_call_target="tpu_custom_call" | custom-call | tf_op jit(solution)/shard_map/pack/pallas_call | solution.py:251
  10.2 6.3 %all-to-all-start = ((bf16[8,136,128]{2,1,0:T(8,128)(2,1)}), bf16[8,136,128]{2,1,0:T(8,128)(2,1)S(1)}, u32[]{:S(2)}, u32[]{:S(2)}) async-start(bf16[8,136,128]{2,1,0:T(8,128)(2,1)} %pack.1), calls=%async_computation | async-start | bytes 557056 | tf_op jit(solution)/shard_map/all_to_all | solution.py:258
  16.8 0.3 multiply_cosine_fusion
  17.1 0.1 pad_maximum_fusion.table_ref
  17.2 8.1 %all-to-all-done.got_ref = bf16[8,136,128]{2,1,0:T(8,128)(2,1)S(1)} async-done(((bf16[8,136,128]{2,1,0:T(8,128)(2,1)}), bf16[8,136,128]{2,1,0:T(8,128)(2,1)S(1)}, u32[]{:S(2)}, u32[]{:S(2)}) %all-to-all-start) | async-done | bytes 278560 | tf_op jit(solution)/shard_map/all_to_all | solution.py:258
  25.3 2.2 %copy-done = bf16[8,2048,128]{2,1,0:T(8,128)(2,1)S(1)} copy-done((bf16[8,2048,128]{2,1,0:T(8,128)(2,1)S(1)}, bf16[8,2048,128]{2,1,0:T(8,128)(2,1)}, u32[]{:S(2)}) %copy-start) | copy-done | bytes 4194328
  27.5 2.2 %copy-done.1 = bf16[8,2048,128]{2,1,0:T(8,128)(2,1)S(1)} copy-done((bf16[8,2048,128]{2,1,0:T(8,128)(2,1)S(1)}, bf16[8,2048,128]{2,1,0:T(8,128)(2,1)}, u32[]{:S(2)}) %copy-start.1) | copy-done | bytes 4194328
  29.7 0.7 %copy-done.3 = s32[8]{0:T(128)S(1)} copy-done((s32[8]{0:T(128)S(1)}, s32[8]{0:T(128)}, u32[]{:S(2)}) %copy-start.3) | copy-done | bytes 56
  30.3 8.8 %attend.1 = (bf16[8,136,128]{2,1,0:T(8,128)(2,1)}, f32[16,256]{1,0:T(8,128)S(1)}) custom-call(s32[8]{0:T(128)S(1)} %copy-done.3, s32[128]{0:T(128)S(1)} %reshape_reshape.4.keep_ref, s32[1]{0:T(128)} %bitcast.rank_ref, f32[8,128]{1,0:T(8,128)S(1)} %broadcast_in_dim.52.base_ref, f32[128,256]{1,0:T(8,128)S(1)} %pad_maximum_fusion.table_ref, ...), custom_call_target="tpu_custom_call" | custom-call | tf_op jit(solution)/shard_map/attend/pallas_call | solution.py:263
  39.1 0.6 %copy-done.2 = f32[16,256]{1,0:T(8,128)} copy-done((f32[16,256]{1,0:T(8,128)}, f32[16,256]{1,0:T(8,128)S(1)}, u32[]{:S(2)}) %copy-start.2) | copy-done | bytes 16408
  39.7 3.6 %all-to-all-start.1 = ((bf16[8,136,128]{2,1,0:T(8,128)(2,1)}), bf16[8,136,128]{2,1,0:T(8,128)(2,1)S(1)}, u32[]{:S(2)}, u32[]{:S(2)}) async-start(bf16[8,136,128]{2,1,0:T(8,128)(2,1)} %get-tuple-element.9), calls=%async_computation.1 | async-start | bytes 557056 | tf_op jit(solution)/shard_map/all_to_all | solution.py:291
  43.3 1.8 %fresh.1 = (f32[128,128]{1,0:T(8,128)}, f32[8,128]{1,0:T(8,128)}) custom-call(bf16[16,1024]{1,0:T(8,128)(2,1)} %bitcast.8, f32[16,256]{1,0:T(8,128)} %copy-done.2, bf16[16,128]{1,0:T(8,128)(2,1)} %bitcast.10, bf16[16,128]{1,0:T(8,128)(2,1)} %bitcast.11), custom_call_target="tpu_custom_call" | custom-call | flops 1048576 | bytes 65536 | tf_op jit(solution)/shard_map/fresh/pallas_call | solution.py:292
  45.1 7.0 %all-to-all-done.1.got_ref = bf16[8,136,128]{2,1,0:T(8,128)(2,1)S(1)} async-done(((bf16[8,136,128]{2,1,0:T(8,128)(2,1)}), bf16[8,136,128]{2,1,0:T(8,128)(2,1)S(1)}, u32[]{:S(2)}, u32[]{:S(2)}) %all-to-all-start.1) | async-done | bytes 278560 | tf_op jit(solution)/shard_map/all_to_all | solution.py:291
  52.1 0.7 %copy-done.4 = bf16[8,136,128]{2,1,0:T(8,128)(2,1)} copy-done((bf16[8,136,128]{2,1,0:T(8,128)(2,1)}, bf16[8,136,128]{2,1,0:T(8,128)(2,1)S(1)}, u32[]{:S(2)}) %copy-start.4) | copy-done | bytes 278552
  52.8 2.0 %merge.1 = bf16[16,1024]{1,0:T(8,128)(2,1)} custom-call(bf16[8,136,128]{2,1,0:T(8,128)(2,1)} %copy-done.4, f32[128,128]{1,0:T(8,128)} %get-tuple-element.11.fresh_ref, f32[8,128]{1,0:T(8,128)} %get-tuple-element.12.note_ref), custom_call_target="tpu_custom_call" | custom-call | tf_op jit(solution)/shard_map/merge/pallas_call | solution.py:305
  (24 shorter events, 0.5 us)
Async XLA Ops:
  2.2 1.6 %collective-permute-start = (f32[8,128]{1,0:T(8,128)S(1)}, f32[8,128]{1,0:T(8,128)S(1)}, u32[]{:S(2)}, u32[]{:S(2)}) collective-permute-start(f32[8,128]{1,0:T(8,128)S(1)} %broadcast_in_dim.55), channel_id=1, source_target_pairs={{0,1},{1,0},{2,3},{3,2},{4,5},{5,4},{6,7},{7,6},{8,9},{9,8},{10,11... | collective-permute-start | bytes 12296 | tf_op jit(solution)/shard_map/ppermute | solution.py:246
  4.0 4.2 %copy-start.5 = (f32[8,128]{1,0:T(8,128)}, f32[8,128]{1,0:T(8,128)S(1)}, u32[]{:S(2)}) copy-start(f32[8,128]{1,0:T(8,128)S(1)} %select_select_fusion.near_ref) | copy-start | bytes 12292
  4.0 4.2 %collective-permute-start.1 = (f32[8,128]{1,0:T(8,128)S(1)}, f32[8,128]{1,0:T(8,128)S(1)}, u32[]{:S(2)}, u32[]{:S(2)}) collective-permute-start(f32[8,128]{1,0:T(8,128)S(1)} %select_select_fusion.near_ref), channel_id=1, source_target_pairs={{0,2},{1,3},{2,0},{3,1},{4,6},{5,7},{6,4},{7,5},{8,10},{9,11},{10,... | collective-permute-start | bytes 12296 | tf_op jit(solution)/shard_map/ppermute | solution.py:249
  8.1 0.6 %copy-start.6 = (f32[8,128]{1,0:T(8,128)}, f32[8,128]{1,0:T(8,128)S(1)}, u32[]{:S(2)}) copy-start(f32[8,128]{1,0:T(8,128)S(1)} %collective-permute-done.1.far_ref) | copy-start | bytes 12292
  10.2 15.1 %all-to-all-start = ((bf16[8,136,128]{2,1,0:T(8,128)(2,1)}), bf16[8,136,128]{2,1,0:T(8,128)(2,1)S(1)}, u32[]{:S(2)}, u32[]{:S(2)}) async-start(bf16[8,136,128]{2,1,0:T(8,128)(2,1)} %pack.1), calls=%async_computation | async-start | bytes 557056 | tf_op jit(solution)/shard_map/all_to_all | solution.py:258
  25.3 2.2 %copy-start = (bf16[8,2048,128]{2,1,0:T(8,128)(2,1)S(1)}, bf16[8,2048,128]{2,1,0:T(8,128)(2,1)}, u32[]{:S(2)}) copy-start(bf16[8,2048,128]{2,1,0:T(8,128)(2,1)} %key_ref.1) | copy-start | bytes 12582916
  27.5 2.2 %copy-start.1 = (bf16[8,2048,128]{2,1,0:T(8,128)(2,1)S(1)}, bf16[8,2048,128]{2,1,0:T(8,128)(2,1)}, u32[]{:S(2)}) copy-start(bf16[8,2048,128]{2,1,0:T(8,128)(2,1)} %value_ref.1) | copy-start | bytes 12582916
  29.7 0.7 %copy-start.3 = (s32[8]{0:T(128)S(1)}, s32[8]{0:T(128)}, u32[]{:S(2)}) copy-start(s32[8]{0:T(128)} %owner_ref.1) | copy-start | bytes 100
  39.1 0.6 %copy-start.2 = (f32[16,256]{1,0:T(8,128)}, f32[16,256]{1,0:T(8,128)S(1)}, u32[]{:S(2)}) copy-start(f32[16,256]{1,0:T(8,128)S(1)} %get-tuple-element.10.own_ref) | copy-start | bytes 49156
  39.7 12.3 %all-to-all-start.1 = ((bf16[8,136,128]{2,1,0:T(8,128)(2,1)}), bf16[8,136,128]{2,1,0:T(8,128)(2,1)S(1)}, u32[]{:S(2)}, u32[]{:S(2)}) async-start(bf16[8,136,128]{2,1,0:T(8,128)(2,1)} %get-tuple-element.9), calls=%async_computation.1 | async-start | bytes 557056 | tf_op jit(solution)/shard_map/all_to_all | solution.py:291
  52.0 0.7 %copy-start.4 = (bf16[8,136,128]{2,1,0:T(8,128)(2,1)}, bf16[8,136,128]{2,1,0:T(8,128)(2,1)S(1)}, u32[]{:S(2)}) copy-start(bf16[8,136,128]{2,1,0:T(8,128)(2,1)S(1)} %all-to-all-done.1.got_ref) | copy-start | bytes 835588

commit v2 on v1

--- a/solution.py
+++ b/solution.py
@@ -33,17 +33,40 @@
     return jnp.concatenate([cosine, cosine, -sine, sine], axis=1)
 
 
+def iota(shape, axis):
+    return lax.broadcasted_iota(jnp.int32, shape, axis)
+
+
 def turned(x, cosine, sine):
     return x * cosine + pltpu.roll(x, x.shape[-1] // 2, x.ndim - 1) * sine
 
 
-def pack_kernel(groups, width, query_ref, near_ref, far_ref, out_ref):
+def count_kernel(keep_ref, count_ref, base_ref):
+    sequences, _, blocks = keep_ref.shape
+    lanes = sequences * blocks
+    me = lax.axis_index("seq")
+    keep = keep_ref[...].reshape(sequences, blocks).astype(F32)
+    spread = lax.rem(iota((blocks, lanes), 1), blocks) == iota((blocks, lanes), 0)
+    wide = jnp.dot(keep, spread.astype(F32), preferred_element_type=F32)
+    mine = iota((sequences, lanes), 1) // blocks == iota((sequences, lanes), 0)
+    flat = jnp.sum(jnp.where(mine, wide, 0.0), axis=0, keepdims=True)
+    flat = jnp.broadcast_to(flat, (EXTRA, lanes))
+    row, col = iota((lanes, lanes), 0), iota((lanes, lanes), 1)
+    same = row // blocks == col // blocks
+    count_ref[...] = jnp.dot(flat, same.astype(F32), preferred_element_type=F32)
+    earlier = jnp.dot(flat, (same & (row < col)).astype(F32), preferred_element_type=F32)
+    block = (lax.rem(iota((EXTRA, lanes), 1), blocks) + me * blocks).astype(F32)
+    base_ref[...] = jnp.where(iota((EXTRA, lanes), 0) == 0, block - earlier, flat)
+
+
+def pack_kernel(groups, width, query_ref, *refs):
+    out_ref = refs[-1]
     steps = query_ref.shape[0]
     rows = groups * steps
     parts = [query_ref[:, g * width : (g + 1) * width] for g in range(groups)]
-    near = near_ref[...]
-    far = far_ref[...]
-    counts = jnp.concatenate([near[0:2], far[0:2], near[4:8]], axis=0).astype(BF)
+    counts = [ref[0:1, :] for ref in refs[:-1]]
+    fill = refs[0][len(counts) : EXTRA, :]
+    counts = jnp.concatenate(counts + [fill], axis=0).astype(BF)
     for target in range(out_ref.shape[0]):
         for g in range(groups):
             out_ref[target, g * steps : (g + 1) * steps, :] = parts[g]
@@ -52,27 +75,46 @@
 
 def attend_kernel(
     sizes,
-    owner_ref,
-    keep_ref,
-    rank_ref,
+    owner_hbm,
     base_ref,
     table_ref,
     step_ref,
     got_ref,
-    key_ref,
-    value_ref,
+    key_hbm,
+    value_hbm,
     out_ref,
     own_ref,
     cos_k,
     sin_k,
     cos_q,
     sin_q,
+    bias,
     score_ref,
+    key_ref,
+    value_ref,
+    owner_ref,
+    owner_sem,
+    key_sem,
+    value_sem,
 ):
     owners, blocks, block, groups, steps, width, heads, chunk = sizes
     rows = groups * steps
-    me = rank_ref[0]
+    me = lax.axis_index("seq")
     lanes = owners * blocks
+    fetch_owner = pltpu.make_async_copy(owner_hbm, owner_ref, owner_sem)
+    fetch_owner.start()
+
+    def fetch(s):
+        return (
+            pltpu.make_async_copy(key_hbm.at[s], key_ref.at[s], key_sem.at[s]),
+            pltpu.make_async_copy(value_hbm.at[s], value_ref.at[s], value_sem.at[s]),
+        )
+
+    @pl.loop(0, owners)
+    def _(s):
+        for copy in fetch(s):
+            copy.start()
+
     before = jnp.zeros((1, lanes), F32)
     total = jnp.zeros((heads, lanes), F32)
     for i in range(owners):
@@ -91,6 +133,9 @@
         )
         cos_to[...] = found[:, 0:width]
         sin_to[...] = found[:, width:]
+    kept = jnp.broadcast_to(base_ref[1:2, :], (lanes, lanes)).T[:, 0:block]
+    bias[...] = jnp.where(kept > 0.5, 0.0, floor_score)
+    fetch_owner.wait()
     step_cos, step_sin = step_ref[:, 0:width], step_ref[:, width:]
     factor = math.log2(math.e) / math.sqrt(width)
     lane = lax.broadcasted_iota(jnp.int32, (rows, width), 1)
@@ -105,8 +150,10 @@
     own_ref[:, width:] = own_sin
 
     @pl.loop(0, owners)
-    def _(o):
-        s = owner_ref[o]
+    def _(s):
+        o = lax.fori_loop(0, owners, lambda i, at: jnp.where(owner_ref[i] == s, i, at), 0)
+        for copy in fetch(s):
+            copy.wait()
         cos_now, sin_now = query_turn(s)
         query = got_ref[o, 0:rows, :].astype(F32).reshape(groups, steps, width)
         swapped = pltpu.roll(query.reshape(rows, width), width // 2, 1)
@@ -130,8 +177,7 @@
             )
             for j in range(per):
                 b = c * per + j
-                bias = jnp.where(keep_ref[s * blocks + b] > 0, 0.0, floor_score)
-                piece = scores[:, j * block : (j + 1) * block] + bias
+                piece = scores[:, j * block : (j + 1) * block] + bias[pl.ds(s * blocks + b, 1), :]
                 score_ref[:, b * block : (b + 1) * block] = piece
                 best = jnp.maximum(best, piece)
         shift = (jnp.max(best, axis=1, keepdims=True) * factor).astype(BF).astype(F32)
@@ -214,7 +260,7 @@
 
 
 VMEM = pl.BlockSpec(memory_space=pltpu.VMEM)
-SMEM = pl.BlockSpec(memory_space=pltpu.SMEM)
+ANY = pl.BlockSpec(memory_space=pl.ANY)
 
 
 def shards(
@@ -225,36 +271,34 @@
     block = tokens_here // blocks
     owners = lax.axis_size("seq")
     heads = lax.axis_size("tp")
-    rank = lax.axis_index("seq")
     steps = step_queries.shape[1]
     groups = step_queries.shape[3] // width
     rows = groups * steps
     lanes = sequences * blocks
+    small = pltpu.CompilerParams(vmem_limit_bytes=8 * 1024 * 1024)
     query = step_queries.reshape(steps, groups * width)
     fresh_keys = new_keys.reshape(steps, width)
     fresh_values = new_values.reshape(steps, width)
 
-    mask = keep_mask.reshape(sequences, blocks)
-    count = jnp.sum(mask, axis=1).astype(F32)
-    slot = jnp.sum(
-        jnp.where(jnp.arange(blocks)[None, :, None] > jnp.arange(blocks)[None, None, :],
-                  mask[:, None, :], 0), axis=2)
-    base = (rank * blocks + jnp.arange(blocks)[None, :] - slot).astype(F32).reshape(1, lanes)
-    base = jnp.broadcast_to(base, (EXTRA, lanes))
-    own = jnp.repeat(count, blocks).reshape(1, lanes)
-    own = jnp.broadcast_to(own, (EXTRA, lanes))
-    other = lax.ppermute(own, "tp", [(i, i ^ 1) for i in range(heads)])
-    row = lax.broadcasted_iota(jnp.int32, (EXTRA, lanes), 0)
-    near = jnp.where(row == 0, own, jnp.where(row == 1, other, 0.0))
-    far = lax.ppermute(near, "tp", [(i, i ^ 2) for i in range(heads)])
-
+    count, base = pl.pallas_call(
+        count_kernel,
+        out_shape=(jax.ShapeDtypeStruct((EXTRA, lanes), F32),) * 2,
+        in_specs=[VMEM],
+        out_specs=(VMEM, VMEM),
+        compiler_params=small,
+        name="count",
+    )(keep_mask.transpose(0, 2, 1))
+    counts = [count] + [
+        lax.ppermute(count, "tp", [(i, i ^ k) for i in range(heads)]) for k in range(1, heads)
+    ]
     payload = pl.pallas_call(
         functools.partial(pack_kernel, groups, width),
         out_shape=jax.ShapeDtypeStruct((owners, rows + EXTRA, width), BF),
-        in_specs=[VMEM] * 3,
+        in_specs=[VMEM] * (1 + heads),
         out_specs=VMEM,
+        compiler_params=small,
         name="pack",
-    )(query, near, far)
+    )(query, *counts)
     got = lax.all_to_all(payload, "seq", split_axis=0, concat_axis=0, tiled=True)
 
     table = turn_table(jnp.arange(owners * blocks) * block, width)
@@ -266,27 +310,32 @@
             jax.ShapeDtypeStruct((owners, rows + EXTRA, width), BF),
             jax.ShapeDtypeStruct((steps, 2 * width), F32),
         ),
-        in_specs=[SMEM, SMEM, SMEM] + [VMEM] * 6,
+        in_specs=[ANY] + [VMEM] * 4 + [ANY] * 2,
         out_specs=(VMEM, VMEM),
         scratch_shapes=[
             pltpu.VMEM((lanes, width), F32),
             pltpu.VMEM((lanes, width), F32),
             pltpu.VMEM((lanes, width), F32),
             pltpu.VMEM((lanes, width), F32),
+            pltpu.VMEM((lanes, block), F32),
             pltpu.VMEM((rows, tokens_here), F32),
+            pltpu.VMEM(prompt_keys.shape, BF),
+            pltpu.VMEM(prompt_values.shape, BF),
+            pltpu.SMEM((owners,), jnp.int32),
+            pltpu.SemaphoreType.DMA,
+            pltpu.SemaphoreType.DMA((owners,)),
+            pltpu.SemaphoreType.DMA((owners,)),
         ],
-        compiler_params=pltpu.CompilerParams(vmem_limit_bytes=40 * 1024 * 1024),
+        compiler_params=pltpu.CompilerParams(vmem_limit_bytes=24000000),
         name="attend",
     )(
-        owner_sequence,
-        mask.reshape(lanes),
-        rank.reshape(1).astype(jnp.int32),
+        pltpu.with_memory_space_constraint(owner_sequence, pltpu.HBM),
         base,
         table,
         step_table,
         got,
-        prompt_keys,
-        prompt_values,
+        pltpu.with_memory_space_constraint(prompt_keys, pltpu.HBM),
+        pltpu.with_memory_space_constraint(prompt_values, pltpu.HBM),
     )
     back = lax.all_to_all(partial, "seq", split_axis=0, concat_axis=0, tiled=True)
     fresh, notes = pl.pallas_call(
@@ -300,6 +349,7 @@
         cost_estimate=pl.CostEstimate(
             flops=4 * rows * steps * width, bytes_accessed=4 * rows * width, transcendentals=0
         ),
+        compiler_params=small,
         name="fresh",
     )(query, own_turn, fresh_keys, fresh_values)
     merged = pl.pallas_call(
@@ -307,6 +357,7 @@
         out_shape=jax.ShapeDtypeStruct((steps, groups * width), BF),
         in_specs=[VMEM] * 3,
         out_specs=VMEM,
+        compiler_params=small,
         name="merge",
     )(back, fresh, notes)
     return merged.reshape(1, steps, 1, groups * width)

time: 55.4 us -> 46.6 us (0.84)
  local copies, waits for them, and re-layouts: 7.76 us -> 1.46 us
  waiting for transfers between devices: 16.6 us -> 19.6 us
  other arithmetic: 3.22 us -> 0.65 us
  Pallas kernels: 14.1 us -> 11.9 us
    unnamed x15 -> x10, local copies, waits for them, and re-layouts: 7.44 us -> 1.46 us
    reduce_sum x2 -> x0, other arithmetic: 2.46 us -> none  [the longest x1 1.57 us: shards(): count = jnp.sum(mask, axis=1).astype(F32)]
    all_to_all x1, waiting for transfers between devices: 6.96 us -> 8.41 us  [shards(): lax.all_to_all(partial, 'seq', split_axis=0, concat_axis=0, tiled=True)]
    pallas_call x1, Pallas kernels: 1.81 us -> 0.42 us  [shards(): pl.pallas_call(functools.partial(fresh_kernel, groups, width), out_shape=...]
    ppermute x2 -> x3, waiting for transfers between devices: 1.58 us -> 2.78 us  [shards(): lax.ppermute(count, 'tp', [(i, i ^ k) for i in range(heads)])]
    pallas_call x1, Pallas kernels: 2 us -> 1.01 us  [shards(): pl.pallas_call(functools.partial(merge_kernel, groups, steps), out_shape=...]
    pallas_call x1, Pallas kernels: 1.52 us -> 0.73 us  [shards(): pl.pallas_call(functools.partial(pack_kernel, groups, width), out_shape=j...]
    pallas_call x1, Pallas kernels: 8.77 us -> 9.5 us  [shards(): pl.pallas_call(functools.partial(attend_kernel, sizes), out_shape=(jax.Sh...]
  transfers between devices with their start and end apart: 4 -> 5, of which waited for: 3 -> 4; matrix products, arithmetic and copies ran while one was open for 3% -> 1% of each run, Pallas kernels for 3% -> 1%
where the time goes in v2:
time: 46.6 us; the launch traced here: 46.2 us
  waiting for transfers between devices  19.6 us (42%)
  starting transfers between devices  12.6 us (27%)
  Pallas kernels  11.9 us (26%)
  local copies, waits for them, and re-layouts  1.46 us (3%)
  other arithmetic  0.65 us (1%)
    pallas_call x1, Pallas kernels, shards(): pl.pallas_call(functools.partial(attend_kernel, sizes), out_shape=(jax.Sh...  9.5 us
    all_to_all x1, waiting for transfers between devices, shards(): lax.all_to_all(partial, 'seq', split_axis=0, concat_axis=0, tiled=True)  8.41 us
    all_to_all x1, waiting for transfers between devices, shards(): lax.all_to_all(payload, 'seq', split_axis=0, concat_axis=0, tiled=True)  8.39 us
    all_to_all x1, starting transfers between devices, shards(): lax.all_to_all(payload, 'seq', split_axis=0, concat_axis=0, tiled=True)  5.81 us
    all_to_all x1, starting transfers between devices, shards(): lax.all_to_all(partial, 'seq', split_axis=0, concat_axis=0, tiled=True)  3.65 us
    ppermute x3, starting transfers between devices, shards(): lax.ppermute(count, 'tp', [(i, i ^ k) for i in range(heads)])  3.11 us
    ppermute x3, waiting for transfers between devices, shards(): lax.ppermute(count, 'tp', [(i, i ^ k) for i in range(heads)])  2.78 us
    unnamed x10, local copies, waits for them, and re-layouts  1.46 us
  transfers between devices with their start and end apart: 5, of which 4 were waited for; matrix products, arithmetic and copies ran while one was open for 1% of the time, Pallas kernels for 1%

profile of v2, /device:TPU:0, one launch (start us, length us, event | category | flops | bytes accessed | tf_op | source)
XLA Modules:
  0.0 46.2 jit_solution(1856382933153944336)
XLA Ops:
  0.0 0.7 %copy-done.4 = s32[8,16,1]{1,2,0:T(1,128)S(1)} copy-done((s32[8,16,1]{1,2,0:T(1,128)S(1)}, s32[8,16,1]{1,2,0:T(1,128)}, u32[]{:S(2)}) %copy-start.4) | copy-done | bytes 536
  0.7 0.2 count.1
  0.9 2.4 %collective-permute-start.2 = (f32[8,128]{1,0:T(8,128)S(1)}, f32[8,128]{1,0:T(8,128)S(1)}, u32[]{:S(2)}, u32[]{:S(2)}) collective-permute-start(f32[8,128]{1,0:T(8,128)S(1)} %get-tuple-element.12.refs_0_), channel_id=1, source_target_pairs={{0,3},{1,2},{2,1},{3,0},{4,7},{5,6},{6,5},{7,4},{8,11},{9,10},{10,... | collective-permute-start | bytes 12296 | tf_op jit(solution)/shard_map/ppermute | solution.py:292
  3.4 0.6 %collective-permute-start.1 = (f32[8,128]{1,0:T(8,128)S(1)}, f32[8,128]{1,0:T(8,128)S(1)}, u32[]{:S(2)}, u32[]{:S(2)}) collective-permute-start(f32[8,128]{1,0:T(8,128)S(1)} %get-tuple-element.12.refs_0_), channel_id=1, source_target_pairs={{0,2},{1,3},{2,0},{3,1},{4,6},{5,7},{6,4},{7,5},{8,10},{9,11},{10,... | collective-permute-start | bytes 12296 | tf_op jit(solution)/shard_map/ppermute | solution.py:292
  3.9 0.1 collective-permute-start
  4.1 0.1 multiply_cosine_fusion.1
  4.2 0.5 %collective-permute-done.2.refs_3_ = f32[8,128]{1,0:T(8,128)S(1)} collective-permute-done((f32[8,128]{1,0:T(8,128)S(1)}, f32[8,128]{1,0:T(8,128)S(1)}, u32[]{:S(2)}, u32[]{:S(2)}) %collective-permute-start.2) | collective-permute-done | bytes 4128 | tf_op jit(solution)/shard_map/ppermute | solution.py:292
  4.7 2.3 %collective-permute-done.1.refs_2_ = f32[8,128]{1,0:T(8,128)S(1)} collective-permute-done((f32[8,128]{1,0:T(8,128)S(1)}, f32[8,128]{1,0:T(8,128)S(1)}, u32[]{:S(2)}, u32[]{:S(2)}) %collective-permute-start.1) | collective-permute-done | bytes 4128 | tf_op jit(solution)/shard_map/ppermute | solution.py:292
  7.0 0.0 collective-permute-done.refs_1_
  7.0 0.8 %copy-done = bf16[1,16,1,1024]{3,1,2,0:T(8,128)(2,1)S(1)} copy-done((bf16[1,16,1,1024]{3,1,2,0:T(8,128)(2,1)S(1)}, bf16[1,16,1,1024]{3,1,2,0:T(8,128)(2,1)}, u32[]{:S(2)}) %copy-start) | copy-done | bytes 32792
  7.7 0.7 %pack.1 = bf16[8,136,128]{2,1,0:T(8,128)(2,1)} custom-call(bf16[16,1024]{1,0:T(8,128)(2,1)S(1)} %bitcast.7, f32[8,128]{1,0:T(8,128)S(1)} %get-tuple-element.12.refs_0_, f32[8,128]{1,0:T(8,128)S(1)} %collective-permute-done.refs_1_, f32[8,128]{1,0:T(8,128)S(1)} %collective-permute-done.1.refs_2_, f32[8,128]{1,0:T(8,128)S(1)} %collective-permute-done.2.refs_3_), custom_call_target="tpu_custom_call" | custom-call | tf_op jit(solution)/shard_map/pack/pallas_call | solution.py:294
  8.5 5.8 %all-to-all-start = ((bf16[8,136,128]{2,1,0:T(8,128)(2,1)}), bf16[8,136,128]{2,1,0:T(8,128)(2,1)S(1)}, u32[]{:S(2)}, u32[]{:S(2)}) async-start(bf16[8,136,128]{2,1,0:T(8,128)(2,1)} %pack.1), calls=%async_computation | async-start | bytes 557056 | tf_op jit(solution)/shard_map/all_to_all | solution.py:302
  14.3 0.1 pad_maximum_fusion.1.step_ref
  14.4 0.3 multiply_cosine_fusion
  14.7 0.1 pad_maximum_fusion.table_ref
  14.8 8.4 %all-to-all-done.got_ref = bf16[8,136,128]{2,1,0:T(8,128)(2,1)S(1)} async-done(((bf16[8,136,128]{2,1,0:T(8,128)(2,1)}), bf16[8,136,128]{2,1,0:T(8,128)(2,1)S(1)}, u32[]{:S(2)}, u32[]{:S(2)}) %all-to-all-start) | async-done | bytes 278560 | tf_op jit(solution)/shard_map/all_to_all | solution.py:302
  23.2 9.5 %attend.1 = (bf16[8,136,128]{2,1,0:T(8,128)(2,1)}, f32[16,256]{1,0:T(8,128)S(1)}) custom-call(s32[8]{0:T(128)} %owner_hbm.1, f32[8,128]{1,0:T(8,128)S(1)} %get-tuple-element.11.base_ref, f32[128,256]{1,0:T(8,128)S(1)} %pad_maximum_fusion.table_ref, f32[16,256]{1,0:T(8,128)S(1)} %pad_maximum_fusion.1.step_ref, bf16[8,136,128]{2,1,0:T(8,128)(2,1)S(1)} %all-to-all-done.got_ref, ...), custom_call_target="tpu_custom_call" | custom-call | tf_op jit(solution)/shard_map/attend/pallas_call | solution.py:307
  32.7 3.6 %all-to-all-start.1 = ((bf16[8,136,128]{2,1,0:T(8,128)(2,1)}), bf16[8,136,128]{2,1,0:T(8,128)(2,1)S(1)}, u32[]{:S(2)}, u32[]{:S(2)}) async-start(bf16[8,136,128]{2,1,0:T(8,128)(2,1)} %get-tuple-element.13), calls=%async_computation.1 | async-start | bytes 557056 | tf_op jit(solution)/shard_map/all_to_all | solution.py:340
  36.3 0.0 copy-done.1
  36.4 0.0 copy-done.2
  36.4 0.0 copy-done.3
  36.4 0.4 fresh.1
  36.8 8.4 %all-to-all-done.1.got_ref = bf16[8,136,128]{2,1,0:T(8,128)(2,1)S(1)} async-done(((bf16[8,136,128]{2,1,0:T(8,128)(2,1)}), bf16[8,136,128]{2,1,0:T(8,128)(2,1)S(1)}, u32[]{:S(2)}, u32[]{:S(2)}) %all-to-all-start.1) | async-done | bytes 278560 | tf_op jit(solution)/shard_map/all_to_all | solution.py:340
  45.2 1.0 %merge.1 = bf16[16,1024]{1,0:T(8,128)(2,1)} custom-call(bf16[8,136,128]{2,1,0:T(8,128)(2,1)S(1)} %all-to-all-done.1.got_ref, f32[128,128]{1,0:T(8,128)S(1)} %get-tuple-element.15.fresh_ref, f32[8,128]{1,0:T(8,128)S(1)} %get-tuple-element.16.note_ref), custom_call_target="tpu_custom_call" | custom-call | tf_op jit(solution)/shard_map/merge/pallas_call | solution.py:355
  (8 shorter events, 0.0 us)
Async XLA Ops:
  0.0 0.7 %copy-start.4 = (s32[8,16,1]{1,2,0:T(1,128)S(1)}, s32[8,16,1]{1,2,0:T(1,128)}, u32[]{:S(2)}) copy-start(s32[8,16,1]{1,2,0:T(1,128)} %param.9) | copy-start | bytes 1540
  0.9 3.8 %collective-permute-start.2 = (f32[8,128]{1,0:T(8,128)S(1)}, f32[8,128]{1,0:T(8,128)S(1)}, u32[]{:S(2)}, u32[]{:S(2)}) collective-permute-start(f32[8,128]{1,0:T(8,128)S(1)} %get-tuple-element.12.refs_0_), channel_id=1, source_target_pairs={{0,3},{1,2},{2,1},{3,0},{4,7},{5,6},{6,5},{7,4},{8,11},{9,10},{10,... | collective-permute-start | bytes 12296 | tf_op jit(solution)/shard_map/ppermute | solution.py:292
  3.4 3.6 %collective-permute-start.1 = (f32[8,128]{1,0:T(8,128)S(1)}, f32[8,128]{1,0:T(8,128)S(1)}, u32[]{:S(2)}, u32[]{:S(2)}) collective-permute-start(f32[8,128]{1,0:T(8,128)S(1)} %get-tuple-element.12.refs_0_), channel_id=1, source_target_pairs={{0,2},{1,3},{2,0},{3,1},{4,6},{5,7},{6,4},{7,5},{8,10},{9,11},{10,... | collective-permute-start | bytes 12296 | tf_op jit(solution)/shard_map/ppermute | solution.py:292
  3.9 3.0 %collective-permute-start = (f32[8,128]{1,0:T(8,128)S(1)}, f32[8,128]{1,0:T(8,128)S(1)}, u32[]{:S(2)}, u32[]{:S(2)}) collective-permute-start(f32[8,128]{1,0:T(8,128)S(1)} %get-tuple-element.12.refs_0_), channel_id=1, source_target_pairs={{0,1},{1,0},{2,3},{3,2},{4,5},{5,4},{6,7},{7,6},{8,9},{9,8},{10,11... | collective-permute-start | bytes 12296 | tf_op jit(solution)/shard_map/ppermute | solution.py:292
  7.0 0.8 %copy-start = (bf16[1,16,1,1024]{3,1,2,0:T(8,128)(2,1)S(1)}, bf16[1,16,1,1024]{3,1,2,0:T(8,128)(2,1)}, u32[]{:S(2)}) copy-start(bf16[1,16,1,1024]{3,1,2,0:T(8,128)(2,1)} %param.11) | copy-start | bytes 98308
  8.5 14.7 %all-to-all-start = ((bf16[8,136,128]{2,1,0:T(8,128)(2,1)}), bf16[8,136,128]{2,1,0:T(8,128)(2,1)S(1)}, u32[]{:S(2)}, u32[]{:S(2)}) async-start(bf16[8,136,128]{2,1,0:T(8,128)(2,1)} %pack.1), calls=%async_computation | async-start | bytes 557056 | tf_op jit(solution)/shard_map/all_to_all | solution.py:302
  23.2 13.2 %copy-start.1 = (bf16[1,16,1,1024]{3,1,2,0:T(8,128)(2,1)S(1)}, bf16[1,16,1,1024]{3,1,2,0:T(8,128)(2,1)}, u32[]{:S(2)}) copy-start(bf16[1,16,1,1024]{3,1,2,0:T(8,128)(2,1)} %param.11) | copy-start | bytes 98308
  23.2 13.2 %copy-start.2 = (bf16[1,16,128]{2,1,0:T(8,128)(2,1)S(1)}, bf16[1,16,128]{2,1,0:T(8,128)(2,1)}, u32[]{:S(2)}) copy-start(bf16[1,16,128]{2,1,0:T(8,128)(2,1)} %param.12) | copy-start | bytes 12292
  23.2 13.2 %copy-start.3 = (bf16[1,16,128]{2,1,0:T(8,128)(2,1)S(1)}, bf16[1,16,128]{2,1,0:T(8,128)(2,1)}, u32[]{:S(2)}) copy-start(bf16[1,16,128]{2,1,0:T(8,128)(2,1)} %param.13) | copy-start | bytes 12292
  32.7 12.5 %all-to-all-start.1 = ((bf16[8,136,128]{2,1,0:T(8,128)(2,1)}), bf16[8,136,128]{2,1,0:T(8,128)(2,1)S(1)}, u32[]{:S(2)}, u32[]{:S(2)}) async-start(bf16[8,136,128]{2,1,0:T(8,128)(2,1)} %get-tuple-element.13), calls=%async_computation.1 | async-start | bytes 557056 | tf_op jit(solution)/shard_map/all_to_all | solution.py:340

commit v3 on v2

--- a/solution.py
+++ b/solution.py
@@ -59,23 +59,29 @@
     base_ref[...] = jnp.where(iota((EXTRA, lanes), 0) == 0, block - earlier, flat)
 
 
-def pack_kernel(groups, width, query_ref, *refs):
+def pack_kernel(query_ref, *refs):
     out_ref = refs[-1]
-    steps = query_ref.shape[0]
-    rows = groups * steps
-    parts = [query_ref[:, g * width : (g + 1) * width] for g in range(groups)]
+    rows = query_ref.shape[0]
+    query = query_ref[...]
     counts = [ref[0:1, :] for ref in refs[:-1]]
     fill = refs[0][len(counts) : EXTRA, :]
     counts = jnp.concatenate(counts + [fill], axis=0).astype(BF)
     for target in range(out_ref.shape[0]):
-        for g in range(groups):
-            out_ref[target, g * steps : (g + 1) * steps, :] = parts[g]
+        out_ref[target, 0:rows, :] = query
         out_ref[target, rows : rows + EXTRA, :] = counts
+
+
+def order_kernel(groups, width, query_ref, out_ref):
+    steps = query_ref.shape[0]
+    for g in range(groups):
+        out_ref[g * steps : (g + 1) * steps, :] = query_ref[:, g * width : (g + 1) * width]
 
 
 def attend_kernel(
     sizes,
     owner_hbm,
+    slot_ref,
+    count_ref,
     base_ref,
     table_ref,
     step_ref,
@@ -88,11 +94,14 @@
     sin_k,
     cos_q,
     sin_q,
-    bias,
-    score_ref,
+    score_a,
+    score_b,
+    best_a,
+    best_b,
     key_ref,
     value_ref,
     owner_ref,
+    place_ref,
     owner_sem,
     key_sem,
     value_sem,
@@ -127,14 +136,17 @@
     pick_k = (entry == dropped).astype(F32)
     pick_q = (entry == longest).astype(F32)
     dims = (((0,), (0,)), ((), ()))
+    table = table_ref[...]
+    parts = []
+    for _ in range(3):
+        part = table.astype(BF)
+        parts.append(part)
+        table = table - part.astype(F32)
     for pick, cos_to, sin_to in ((pick_k, cos_k, sin_k), (pick_q, cos_q, sin_q)):
-        found = lax.dot_general(
-            pick, table_ref[...], dims, precision=HIGH, preferred_element_type=F32
-        )
+        pick = pick.T.astype(BF)
+        found = sum(jnp.dot(pick, part, preferred_element_type=F32) for part in parts[::-1])
         cos_to[...] = found[:, 0:width]
         sin_to[...] = found[:, width:]
-    kept = jnp.broadcast_to(base_ref[1:2, :], (lanes, lanes)).T[:, 0:block]
-    bias[...] = jnp.where(kept > 0.5, 0.0, floor_score)
     fetch_owner.wait()
     step_cos, step_sin = step_ref[:, 0:width], step_ref[:, width:]
     factor = math.log2(math.e) / math.sqrt(width)
@@ -149,57 +161,88 @@
     own_ref[:, 0:width] = own_cos
     own_ref[:, width:] = own_sin
 
+    per = chunk // block
+
     @pl.loop(0, owners)
-    def _(s):
-        o = lax.fori_loop(0, owners, lambda i, at: jnp.where(owner_ref[i] == s, i, at), 0)
-        for copy in fetch(s):
-            copy.wait()
-        cos_now, sin_now = query_turn(s)
-        query = got_ref[o, 0:rows, :].astype(F32).reshape(groups, steps, width)
-        swapped = pltpu.roll(query.reshape(rows, width), width // 2, 1)
-        query = query * cos_now[None] + swapped.reshape(groups, steps, width) * sin_now[None]
-        query = query.reshape(rows, width).astype(BF)
-        best = jnp.full((rows, width), floor_score, F32)
-        per = chunk // block
+    def _(i):
+        place_ref[owner_ref[i]] = i
+
+    def step_over(ahead, fill, behind, drain):
+        if ahead is not None:
+            cos_now, sin_now = query_turn(ahead)
+            query = got_ref[place_ref[ahead], 0:rows, :].astype(F32)
+            swapped = pltpu.roll(query, width // 2, 1).reshape(groups, steps, width)
+            query = query.reshape(groups, steps, width) * cos_now[None] + swapped * sin_now[None]
+            query = query.reshape(rows, width).astype(BF)
+            best = jnp.full((rows, block), -jnp.inf, F32)
+        if behind is not None:
+            scores_in, best_in = drain
+            held = count_ref[behind]
+            shift = (jnp.max(best_in[...], axis=1, keepdims=True) * factor).astype(BF).astype(F32)
+            result = jnp.zeros((rows, 2 * width), F32)
         for c in range(blocks // per):
-            keys = []
-            for j in range(per):
-                b = c * per + j
-                cosine = cos_k[pl.ds(s * blocks + b, 1), :]
-                sine = sin_k[pl.ds(s * blocks + b, 1), :]
-                x = key_ref[s, b * block : (b + 1) * block, :].astype(F32)
-                keys.append(turned(x, cosine, -sine).astype(BF))
-            scores = lax.dot_general(
-                query,
-                jnp.concatenate(keys, axis=0),
-                (((1,), (1,)), ((), ())),
-                preferred_element_type=F32,
-            )
-            for j in range(per):
-                b = c * per + j
-                piece = scores[:, j * block : (j + 1) * block] + bias[pl.ds(s * blocks + b, 1), :]
-                score_ref[:, b * block : (b + 1) * block] = piece
-                best = jnp.maximum(best, piece)
-        shift = (jnp.max(best, axis=1, keepdims=True) * factor).astype(BF).astype(F32)
-        sums = jnp.zeros((rows, block), F32)
-        result = jnp.zeros((rows, width), F32)
-        for c in range(blocks // per):
-            weights = []
-            for j in range(per):
-                b = c * per + j
-                w = jnp.exp2(score_ref[:, b * block : (b + 1) * block] * factor - shift)
-                sums = sums + w
-                weights.append(w.astype(BF))
-            result = result + jnp.dot(
-                jnp.concatenate(weights, axis=1),
-                value_ref[s, c * chunk : (c + 1) * chunk, :],
-                preferred_element_type=F32,
-            )
-        mass = jnp.sum(sums, axis=1, keepdims=True)
-        high = mass.astype(BF).astype(F32)
-        notes = jnp.where(lane == 0, shift, jnp.where(lane == 1, high, mass - high))
-        out_ref[o, 0:rows, :] = result.astype(BF)
-        out_ref[o, rows : rows + EXTRA, :] = notes.T[0:EXTRA].astype(BF)
+            slots = range(c * per, (c + 1) * per)
+            if ahead is not None:
+                scores_out, best_out = fill
+                keys = []
+                for r in slots:
+                    b = slot_ref[ahead * blocks + r]
+                    cosine = cos_k[pl.ds(ahead * blocks + b, 1), :]
+                    sine = sin_k[pl.ds(ahead * blocks + b, 1), :]
+                    x = key_ref[ahead, pl.ds(pl.multiple_of(b * block, block), block), :]
+                    keys.append(turned(x.astype(F32), cosine, -sine).astype(BF))
+                scores = lax.dot_general(
+                    query,
+                    jnp.concatenate(keys, axis=0),
+                    (((1,), (1,)), ((), ())),
+                    preferred_element_type=F32,
+                )
+                scores_out[:, c * chunk : (c + 1) * chunk] = scores
+                for j in range(per):
+                    best = jnp.maximum(best, scores[:, j * block : (j + 1) * block])
+            if behind is not None:
+                weights = jnp.exp2(scores_in[:, c * chunk : (c + 1) * chunk] * factor - shift)
+                values = []
+                for r in slots:
+                    b = slot_ref[behind * blocks + r]
+                    live = jnp.where(r < held, 1.0, 0.0).astype(F32)
+                    live = jnp.full((block, width), live, F32).astype(BF)
+                    v = value_ref[behind, pl.ds(pl.multiple_of(b * block, block), block), :]
+                    values.append(jnp.concatenate([v * live, live], axis=1))
+                result = result + jnp.dot(
+                    weights.astype(BF),
+                    jnp.concatenate(values, axis=0),
+                    preferred_element_type=F32,
+                )
+        if ahead is not None:
+            best_out[...] = best
+        if behind is not None:
+            o = place_ref[behind]
+            shift = jnp.where(held > 0, shift, floor_score)
+            mass = result[:, width:]
+            high = mass.astype(BF).astype(F32)
+            notes = jnp.where(lane == 0, shift, jnp.where(lane == 1, high, mass - high))
+            out_ref[o, 0:rows, :] = result[:, 0:width].astype(BF)
+            out_ref[o, rows : rows + EXTRA, :] = notes.T[0:EXTRA].astype(BF)
+
+    even, odd = (score_a, best_a), (score_b, best_b)
+    fetch(0)[0].wait()
+    step_over(0, even, None, None)
+
+    @pl.loop(0, owners // 2 - 1)
+    def _(i):
+        fetch(2 * i + 1)[0].wait()
+        fetch(2 * i + 2)[0].wait()
+        fetch(2 * i)[1].wait()
+        fetch(2 * i + 1)[1].wait()
+        step_over(2 * i + 1, odd, 2 * i, even)
+        step_over(2 * i + 2, even, 2 * i + 1, odd)
+
+    fetch(owners - 1)[0].wait()
+    fetch(owners - 2)[1].wait()
+    fetch(owners - 1)[1].wait()
+    step_over(owners - 1, odd, owners - 2, even)
+    step_over(None, None, owners - 1, odd)
 
 
 def fresh_kernel(groups, width, query_ref, own_ref, key_ref, value_ref, out_ref, note_ref):
@@ -261,6 +304,50 @@
 
 VMEM = pl.BlockSpec(memory_space=pltpu.VMEM)
 ANY = pl.BlockSpec(memory_space=pl.ANY)
+SMEM = pl.BlockSpec(memory_space=pltpu.SMEM)
+
+
+def attend(sizes, owner, slots, held, base, table, step_table, got, keys, values, **kw):
+    owners, blocks, block, groups, steps, width, heads, chunk = sizes
+    rows, lanes = groups * steps, owners * blocks
+    return pl.pallas_call(
+        functools.partial(attend_kernel, sizes, **kw),
+        out_shape=(
+            jax.ShapeDtypeStruct((owners, rows + EXTRA, width), BF),
+            jax.ShapeDtypeStruct((steps, 2 * width), F32),
+        ),
+        in_specs=[ANY] + [SMEM] * 2 + [VMEM] * 4 + [ANY] * 2,
+        out_specs=(VMEM, VMEM),
+        scratch_shapes=[
+            pltpu.VMEM((lanes, width), F32),
+            pltpu.VMEM((lanes, width), F32),
+            pltpu.VMEM((lanes, width), F32),
+            pltpu.VMEM((lanes, width), F32),
+            pltpu.VMEM((rows, blocks * block), F32),
+            pltpu.VMEM((rows, blocks * block), F32),
+            pltpu.VMEM((rows, block), F32),
+            pltpu.VMEM((rows, block), F32),
+            pltpu.VMEM(keys.shape, BF),
+            pltpu.VMEM(values.shape, BF),
+            pltpu.SMEM((owners,), jnp.int32),
+            pltpu.SMEM((owners,), jnp.int32),
+            pltpu.SemaphoreType.DMA,
+            pltpu.SemaphoreType.DMA((owners,)),
+            pltpu.SemaphoreType.DMA((owners,)),
+        ],
+        compiler_params=pltpu.CompilerParams(vmem_limit_bytes=24 * 1024 * 1024),
+        name="attend",
+    )(
+        pltpu.with_memory_space_constraint(owner, pltpu.HBM),
+        slots,
+        held,
+        base,
+        table,
+        step_table,
+        got,
+        pltpu.with_memory_space_constraint(keys, pltpu.HBM),
+        pltpu.with_memory_space_constraint(values, pltpu.HBM),
+    )
 
 
 def shards(
@@ -291,51 +378,39 @@
     counts = [count] + [
         lax.ppermute(count, "tp", [(i, i ^ k) for i in range(heads)]) for k in range(1, heads)
     ]
+    ordered = pl.pallas_call(
+        functools.partial(order_kernel, groups, width),
+        out_shape=jax.ShapeDtypeStruct((rows, width), BF),
+        in_specs=[VMEM],
+        out_specs=VMEM,
+        compiler_params=small,
+        cost_estimate=pl.CostEstimate(
+            flops=rows * width, bytes_accessed=4 * rows * width, transcendentals=0
+        ),
+        name="order",
+    )(query)
     payload = pl.pallas_call(
-        functools.partial(pack_kernel, groups, width),
+        pack_kernel,
         out_shape=jax.ShapeDtypeStruct((owners, rows + EXTRA, width), BF),
         in_specs=[VMEM] * (1 + heads),
         out_specs=VMEM,
         compiler_params=small,
         name="pack",
-    )(query, *counts)
+    )(ordered, *counts)
     got = lax.all_to_all(payload, "seq", split_axis=0, concat_axis=0, tiled=True)
 
+    mask = keep_mask.reshape(sequences, blocks)
+    number = jnp.arange(blocks)
+    rank = jnp.sum(jnp.where(number[None, :] < number[:, None], mask[:, None, :], 0), axis=2)
+    held = jnp.sum(mask, axis=1)
+    wanted = jnp.minimum(number[None, :], held[:, None] - 1)
+    found = (rank[:, None, :] == wanted[:, :, None]) & (mask[:, None, :] > 0)
+    slots = jnp.sum(jnp.where(found, number[None, None, :], 0), axis=2).reshape(lanes)
     table = turn_table(jnp.arange(owners * blocks) * block, width)
     step_table = turn_table(jnp.arange(steps), width)
     sizes = (owners, blocks, block, groups, steps, width, heads, min(4, blocks) * block)
-    partial, own_turn = pl.pallas_call(
-        functools.partial(attend_kernel, sizes),
-        out_shape=(
-            jax.ShapeDtypeStruct((owners, rows + EXTRA, width), BF),
-            jax.ShapeDtypeStruct((steps, 2 * width), F32),
-        ),
-        in_specs=[ANY] + [VMEM] * 4 + [ANY] * 2,
-        out_specs=(VMEM, VMEM),
-        scratch_shapes=[
-            pltpu.VMEM((lanes, width), F32),
-            pltpu.VMEM((lanes, width), F32),
-            pltpu.VMEM((lanes, width), F32),
-            pltpu.VMEM((lanes, width), F32),
-            pltpu.VMEM((lanes, block), F32),
-            pltpu.VMEM((rows, tokens_here), F32),
-            pltpu.VMEM(prompt_keys.shape, BF),
-            pltpu.VMEM(prompt_values.shape, BF),
-            pltpu.SMEM((owners,), jnp.int32),
-            pltpu.SemaphoreType.DMA,
-            pltpu.SemaphoreType.DMA((owners,)),
-            pltpu.SemaphoreType.DMA((owners,)),
-        ],
-        compiler_params=pltpu.CompilerParams(vmem_limit_bytes=24000000),
-        name="attend",
-    )(
-        pltpu.with_memory_space_constraint(owner_sequence, pltpu.HBM),
-        base,
-        table,
-        step_table,
-        got,
-        pltpu.with_memory_space_constraint(prompt_keys, pltpu.HBM),
-        pltpu.with_memory_space_constraint(prompt_values, pltpu.HBM),
+    partial, own_turn = attend(
+        sizes, owner_sequence, slots, held, base, table, step_table, got, prompt_keys, prompt_values
     )
     back = lax.all_to_all(partial, "seq", split_axis=0, concat_axis=0, tiled=True)
     fresh, notes = pl.pallas_call(

time: 46.6 us -> 46.8 us (level)
  other arithmetic: 0.65 us -> 3.53 us
  waiting for transfers between devices: 19.6 us -> 17.7 us
  Pallas kernels: 11.9 us -> 10.6 us
    ppermute x3, waiting for transfers between devices: 2.78 us -> 0.01 us  [shards(): lax.ppermute(count, 'tp', [(i, i ^ k) for i in range(heads)])]
    reduce_sum x0 -> x3, other arithmetic: none -> 2.1 us  [the longest x1 0.92 us: shards(): held = jnp.sum(mask, axis=1)]
    pallas_call x2 -> x3, Pallas kernels: 10.2 us -> 8.93 us  [the longest x1 8.18 us: attend(): pl.pallas_call(functools.partial(attend_kernel, sizes, **kw), out_shape=(...]
    gt x0 -> x1, other arithmetic: none -> 0.7 us  [shards(): found = (rank[:, None, :] == wanted[:, :, None]) & (mask[:, None, :] > 0)]
    all_to_all x1, waiting for transfers between devices: 8.39 us -> 8.95 us  [shards(): lax.all_to_all(payload, 'seq', split_axis=0, concat_axis=0, tiled=True)]
  transfers between devices with their start and end apart: 5 -> 5, of which waited for: 4 -> 2; matrix products, arithmetic and copies ran while one was open for 1% -> 8% of each run, Pallas kernels for 1% -> 1%
where the time goes in v3:
time: 46.8 us; the launch traced here: 46.3 us
  waiting for transfers between devices  17.7 us (38%)
  starting transfers between devices  12.8 us (27%)
  Pallas kernels  10.6 us (23%)
  other arithmetic  3.53 us (8%)
  local copies, waits for them, and re-layouts  1.53 us (3%)
    all_to_all x1, waiting for transfers between devices, shards(): lax.all_to_all(payload, 'seq', split_axis=0, concat_axis=0, tiled=True)  8.95 us
    all_to_all x1, waiting for transfers between devices, shards(): lax.all_to_all(partial, 'seq', split_axis=0, concat_axis=0, tiled=True)  8.77 us
    pallas_call x1, Pallas kernels, attend(): pl.pallas_call(functools.partial(attend_kernel, sizes, **kw), out_shape=(...  8.18 us
    all_to_all x1, starting transfers between devices, shards(): lax.all_to_all(payload, 'seq', split_axis=0, concat_axis=0, tiled=True)  6.03 us
    all_to_all x1, starting transfers between devices, shards(): lax.all_to_all(partial, 'seq', split_axis=0, concat_axis=0, tiled=True)  3.65 us
    ppermute x3, starting transfers between devices, shards(): lax.ppermute(count, 'tp', [(i, i ^ k) for i in range(heads)])  3.11 us
    unnamed x10, local copies, waits for them, and re-layouts  1.45 us
    pallas_call x1, Pallas kernels, shards(): pl.pallas_call(functools.partial(merge_kernel, groups, steps), out_shape=...  1.01 us
  transfers between devices with their start and end apart: 5, of which 2 were waited for; matrix products, arithmetic and copies ran while one was open for 8% of the time, Pallas kernels for 1%

profile of v3, /device:TPU:0, one launch (start us, length us, event | category | flops | bytes accessed | tf_op | source)
XLA Modules:
  0.0 46.3 jit_solution(2308916347497296035)
XLA Ops:
  0.0 0.7 %copy-done.2 = s32[8,16,1]{1,2,0:T(1,128)S(1)} copy-done((s32[8,16,1]{1,2,0:T(1,128)S(1)}, s32[8,16,1]{1,2,0:T(1,128)}, u32[]{:S(2)}) %copy-start.2) | copy-done | bytes 536
  0.7 0.2 count.1
  0.9 2.4 %collective-permute-start.2 = (f32[8,128]{1,0:T(8,128)S(1)}, f32[8,128]{1,0:T(8,128)S(1)}, u32[]{:S(2)}, u32[]{:S(2)}) collective-permute-start(f32[8,128]{1,0:T(8,128)S(1)} %get-tuple-element.12.refs_0_), channel_id=1, source_target_pairs={{0,3},{1,2},{2,1},{3,0},{4,7},{5,6},{6,5},{7,4},{8,11},{9,10},{10,... | collective-permute-start | bytes 12296 | tf_op jit(solution)/shard_map/ppermute | solution.py:379
  3.4 0.6 %collective-permute-start.1 = (f32[8,128]{1,0:T(8,128)S(1)}, f32[8,128]{1,0:T(8,128)S(1)}, u32[]{:S(2)}, u32[]{:S(2)}) collective-permute-start(f32[8,128]{1,0:T(8,128)S(1)} %get-tuple-element.12.refs_0_), channel_id=1, source_target_pairs={{0,2},{1,3},{2,0},{3,1},{4,6},{5,7},{6,4},{7,5},{8,10},{9,11},{10,... | collective-permute-start | bytes 12296 | tf_op jit(solution)/shard_map/ppermute | solution.py:379
  3.9 0.1 collective-permute-start
  4.1 0.9 %reduce_sum.28.count_ref = s32[8]{0:T(128)S(1)} reduce(s32[8,16,1]{1,2,0:T(1,128)} %param.9, s32[]{:T(128)} %constant.7.clone.1), dimensions={1,2}, to_apply=%region_1.2 | reduce | flops 120 | bytes 548 | tf_op jit(solution)/shard_map/reduce_sum | solution.py:405
  5.0 0.7 %broadcast_compare_fusion = pred[8,16]{1,0:T(8,128)(4,1)S(1)} fusion(s32[8,16]{1,0:T(8,128)} %bitcast.10), kind=kLoop, calls=%fused_computation.12 | loop fusion | flops 128 | bytes 640 | tf_op jit(solution)/shard_map/gt | solution.py:407
  5.7 0.9 %select_reduce_fusion.1 = s32[8,16]{1,0:T(8,128)S(1)} fusion(s32[8,16]{1,0:T(8,128)} %bitcast.11, pred[16,16]{1,0:T(8,128)(4,1)S(1)} %iota_compare_fusion), kind=kLoop, calls=%fused_computation.4 | loop fusion | flops 3968 | bytes 1280 | tf_op jit(solution)/shard_map/reduce_sum | solution.py:404
  6.6 0.1 iota_minimum_fusion
  6.7 0.1 multiply_cosine_fusion.1
  6.8 0.3 select_reduce_fusion
  7.1 0.8 %copy-done = bf16[1,16,1,1024]{3,1,2,0:T(8,128)(2,1)S(1)} copy-done((bf16[1,16,1,1024]{3,1,2,0:T(8,128)(2,1)S(1)}, bf16[1,16,1,1024]{3,1,2,0:T(8,128)(2,1)}, u32[]{:S(2)}) %copy-start) | copy-done | bytes 32792
  7.9 0.7 %pack.1 = bf16[8,136,128]{2,1,0:T(8,128)(2,1)} custom-call(bf16[128,128]{1,0:T(8,128)(2,1)S(1)} %order.1.query_ref, f32[8,128]{1,0:T(8,128)S(1)} %get-tuple-element.12.refs_0_, f32[8,128]{1,0:T(8,128)S(1)} %collective-permute-done.refs_1_, f32[8,128]{1,0:T(8,128)S(1)} %collective-permute-done.1.refs_2_, f32[8,128]{1,0:T(8,128)S(1)} %collective-permute-done.2.refs_3_), custom_call_target="tpu_custom_call" | custom-call | tf_op jit(solution)/shard_map/pack/pallas_call | solution.py:392
  8.6 6.0 %all-to-all-start = ((bf16[8,136,128]{2,1,0:T(8,128)(2,1)}), bf16[8,136,128]{2,1,0:T(8,128)(2,1)S(1)}, u32[]{:S(2)}, u32[]{:S(2)}) async-start(bf16[8,136,128]{2,1,0:T(8,128)(2,1)} %pack.1), calls=%async_computation | async-start | bytes 557056 | tf_op jit(solution)/shard_map/all_to_all | solution.py:400
  14.7 0.1 reshape.79.slot_ref
  14.8 0.1 pad_maximum_fusion.1.step_ref
  14.8 0.3 multiply_cosine_fusion
  15.2 0.1 pad_maximum_fusion.table_ref
  15.3 8.9 %all-to-all-done.got_ref = bf16[8,136,128]{2,1,0:T(8,128)(2,1)S(1)} async-done(((bf16[8,136,128]{2,1,0:T(8,128)(2,1)}), bf16[8,136,128]{2,1,0:T(8,128)(2,1)S(1)}, u32[]{:S(2)}, u32[]{:S(2)}) %all-to-all-start) | async-done | bytes 278560 | tf_op jit(solution)/shard_map/all_to_all | solution.py:400
  24.2 8.2 %attend.1 = (bf16[8,136,128]{2,1,0:T(8,128)(2,1)}, f32[16,256]{1,0:T(8,128)S(1)}) custom-call(s32[8]{0:T(128)} %owner_hbm.1, s32[128]{0:T(128)S(1)} %reshape.79.slot_ref, s32[8]{0:T(128)S(1)} %reduce_sum.28.count_ref, f32[8,128]{1,0:T(8,128)S(1)} %get-tuple-element.11.base_ref, f32[128,256]{1,0:T(8,128)S(1)} %pad_maximum_fusion.table_ref, ...), custom_call_target="tpu_custom_call" | custom-call | tf_op jit(solution)/shard_map/attend/pallas_call | solution.py:313
  32.4 3.6 %all-to-all-start.1 = ((bf16[8,136,128]{2,1,0:T(8,128)(2,1)}), bf16[8,136,128]{2,1,0:T(8,128)(2,1)S(1)}, u32[]{:S(2)}, u32[]{:S(2)}) async-start(bf16[8,136,128]{2,1,0:T(8,128)(2,1)} %get-tuple-element.13), calls=%async_computation.1 | async-start | bytes 557056 | tf_op jit(solution)/shard_map/all_to_all | solution.py:415
  36.1 0.4 fresh.1
  36.5 8.8 %all-to-all-done.1.got_ref = bf16[8,136,128]{2,1,0:T(8,128)(2,1)S(1)} async-done(((bf16[8,136,128]{2,1,0:T(8,128)(2,1)}), bf16[8,136,128]{2,1,0:T(8,128)(2,1)S(1)}, u32[]{:S(2)}, u32[]{:S(2)}) %all-to-all-start.1) | async-done | bytes 278560 | tf_op jit(solution)/shard_map/all_to_all | solution.py:415
  45.3 1.0 %merge.1 = bf16[16,1024]{1,0:T(8,128)(2,1)} custom-call(bf16[8,136,128]{2,1,0:T(8,128)(2,1)S(1)} %all-to-all-done.1.got_ref, f32[128,128]{1,0:T(8,128)S(1)} %get-tuple-element.15.fresh_ref, f32[8,128]{1,0:T(8,128)S(1)} %get-tuple-element.16.note_ref), custom_call_target="tpu_custom_call" | custom-call | tf_op jit(solution)/shard_map/merge/pallas_call | solution.py:430
  (17 shorter events, 0.1 us)
Async XLA Ops:
  0.0 0.7 %copy-start.2 = (s32[8,16,1]{1,2,0:T(1,128)S(1)}, s32[8,16,1]{1,2,0:T(1,128)}, u32[]{:S(2)}) copy-start(s32[8,16,1]{1,2,0:T(1,128)} %param.9) | copy-start | bytes 1540
  0.9 6.9 %collective-permute-start.2 = (f32[8,128]{1,0:T(8,128)S(1)}, f32[8,128]{1,0:T(8,128)S(1)}, u32[]{:S(2)}, u32[]{:S(2)}) collective-permute-start(f32[8,128]{1,0:T(8,128)S(1)} %get-tuple-element.12.refs_0_), channel_id=1, source_target_pairs={{0,3},{1,2},{2,1},{3,0},{4,7},{5,6},{6,5},{7,4},{8,11},{9,10},{10,... | collective-permute-start | bytes 12296 | tf_op jit(solution)/shard_map/ppermute | solution.py:379
  3.4 4.5 %collective-permute-start.1 = (f32[8,128]{1,0:T(8,128)S(1)}, f32[8,128]{1,0:T(8,128)S(1)}, u32[]{:S(2)}, u32[]{:S(2)}) collective-permute-start(f32[8,128]{1,0:T(8,128)S(1)} %get-tuple-element.12.refs_0_), channel_id=1, source_target_pairs={{0,2},{1,3},{2,0},{3,1},{4,6},{5,7},{6,4},{7,5},{8,10},{9,11},{10,... | collective-permute-start | bytes 12296 | tf_op jit(solution)/shard_map/ppermute | solution.py:379
  3.9 4.0 %collective-permute-start = (f32[8,128]{1,0:T(8,128)S(1)}, f32[8,128]{1,0:T(8,128)S(1)}, u32[]{:S(2)}, u32[]{:S(2)}) collective-permute-start(f32[8,128]{1,0:T(8,128)S(1)} %get-tuple-element.12.refs_0_), channel_id=1, source_target_pairs={{0,1},{1,0},{2,3},{3,2},{4,5},{5,4},{6,7},{7,6},{8,9},{9,8},{10,11... | collective-permute-start | bytes 12296 | tf_op jit(solution)/shard_map/ppermute | solution.py:379
  7.1 0.8 %copy-start = (bf16[1,16,1,1024]{3,1,2,0:T(8,128)(2,1)S(1)}, bf16[1,16,1,1024]{3,1,2,0:T(8,128)(2,1)}, u32[]{:S(2)}) copy-start(bf16[1,16,1,1024]{3,1,2,0:T(8,128)(2,1)} %param.11) | copy-start | bytes 98308
  8.6 15.6 %all-to-all-start = ((bf16[8,136,128]{2,1,0:T(8,128)(2,1)}), bf16[8,136,128]{2,1,0:T(8,128)(2,1)S(1)}, u32[]{:S(2)}, u32[]{:S(2)}) async-start(bf16[8,136,128]{2,1,0:T(8,128)(2,1)} %pack.1), calls=%async_computation | async-start | bytes 557056 | tf_op jit(solution)/shard_map/all_to_all | solution.py:400
  24.2 11.8 %copy-start.1 = (bf16[1,16,1,1024]{3,1,2,0:T(8,128)(2,1)S(1)}, bf16[1,16,1,1024]{3,1,2,0:T(8,128)(2,1)}, u32[]{:S(2)}) copy-start(bf16[1,16,1,1024]{3,1,2,0:T(8,128)(2,1)} %param.11) | copy-start | bytes 98308
  24.2 11.8 %copy-start.3 = (bf16[1,16,128]{2,1,0:T(8,128)(2,1)S(1)}, bf16[1,16,128]{2,1,0:T(8,128)(2,1)}, u32[]{:S(2)}) copy-start(bf16[1,16,128]{2,1,0:T(8,128)(2,1)} %param.12) | copy-start | bytes 12292
  24.2 11.9 %copy-start.4 = (bf16[1,16,128]{2,1,0:T(8,128)(2,1)S(1)}, bf16[1,16,128]{2,1,0:T(8,128)(2,1)}, u32[]{:S(2)}) copy-start(bf16[1,16,128]{2,1,0:T(8,128)(2,1)} %param.13) | copy-start | bytes 12292
  32.4 12.9 %all-to-all-start.1 = ((bf16[8,136,128]{2,1,0:T(8,128)(2,1)}), bf16[8,136,128]{2,1,0:T(8,128)(2,1)S(1)}, u32[]{:S(2)}, u32[]{:S(2)}) async-start(bf16[8,136,128]{2,1,0:T(8,128)(2,1)} %get-tuple-element.13), calls=%async_computation.1 | async-start | bytes 557056 | tf_op jit(solution)/shard_map/all_to_all | solution.py:415

commit v4 on v3

--- a/solution.py
+++ b/solution.py
@@ -59,6 +59,21 @@
     base_ref[...] = jnp.where(iota((EXTRA, lanes), 0) == 0, block - earlier, flat)
 
 
+def slot_kernel(blocks, count_ref, base_ref, out_ref):
+    lanes = count_ref.shape[1]
+    me = lax.axis_index("seq")
+    row, col = iota((lanes, lanes), 0), iota((lanes, lanes), 1)
+    block = (lax.rem(col, blocks) + me * blocks).astype(F32)
+    rank = block - base_ref[0:1, :]
+    rank = jnp.where(base_ref[1:2, :] > 0.5, rank, -2.0).T
+    held = count_ref[0:1, :]
+    wanted = jnp.minimum(lax.rem(col, blocks).astype(F32), held - 1.0)
+    found = (row // blocks == col // blocks) & (rank == wanted)
+    slots = jnp.sum(jnp.where(found, lax.rem(row, blocks), 0), axis=0, keepdims=True)
+    out_ref[0:1, :] = slots
+    out_ref[1:2, :] = held.astype(jnp.int32)
+
+
 def pack_kernel(query_ref, *refs):
     out_ref = refs[-1]
     rows = query_ref.shape[0]
@@ -81,7 +96,6 @@
     sizes,
     owner_hbm,
     slot_ref,
-    count_ref,
     base_ref,
     table_ref,
     step_ref,
@@ -177,7 +191,7 @@
             best = jnp.full((rows, block), -jnp.inf, F32)
         if behind is not None:
             scores_in, best_in = drain
-            held = count_ref[behind]
+            held = slot_ref[1, behind * blocks]
             shift = (jnp.max(best_in[...], axis=1, keepdims=True) * factor).astype(BF).astype(F32)
             result = jnp.zeros((rows, 2 * width), F32)
         for c in range(blocks // per):
@@ -186,7 +200,7 @@
                 scores_out, best_out = fill
                 keys = []
                 for r in slots:
-                    b = slot_ref[ahead * blocks + r]
+                    b = slot_ref[0, ahead * blocks + r]
                     cosine = cos_k[pl.ds(ahead * blocks + b, 1), :]
                     sine = sin_k[pl.ds(ahead * blocks + b, 1), :]
                     x = key_ref[ahead, pl.ds(pl.multiple_of(b * block, block), block), :]
@@ -204,7 +218,7 @@
                 weights = jnp.exp2(scores_in[:, c * chunk : (c + 1) * chunk] * factor - shift)
                 values = []
                 for r in slots:
-                    b = slot_ref[behind * blocks + r]
+                    b = slot_ref[0, behind * blocks + r]
                     live = jnp.where(r < held, 1.0, 0.0).astype(F32)
                     live = jnp.full((block, width), live, F32).astype(BF)
                     v = value_ref[behind, pl.ds(pl.multiple_of(b * block, block), block), :]
@@ -307,7 +321,7 @@
 SMEM = pl.BlockSpec(memory_space=pltpu.SMEM)
 
 
-def attend(sizes, owner, slots, held, base, table, step_table, got, keys, values, **kw):
+def attend(sizes, owner, slots, base, table, step_table, got, keys, values, **kw):
     owners, blocks, block, groups, steps, width, heads, chunk = sizes
     rows, lanes = groups * steps, owners * blocks
     return pl.pallas_call(
@@ -316,7 +330,7 @@
             jax.ShapeDtypeStruct((owners, rows + EXTRA, width), BF),
             jax.ShapeDtypeStruct((steps, 2 * width), F32),
         ),
-        in_specs=[ANY] + [SMEM] * 2 + [VMEM] * 4 + [ANY] * 2,
+        in_specs=[ANY] + [SMEM] + [VMEM] * 4 + [ANY] * 2,
         out_specs=(VMEM, VMEM),
         scratch_shapes=[
             pltpu.VMEM((lanes, width), F32),
@@ -340,7 +354,6 @@
     )(
         pltpu.with_memory_space_constraint(owner, pltpu.HBM),
         slots,
-        held,
         base,
         table,
         step_table,
@@ -397,20 +410,25 @@
         compiler_params=small,
         name="pack",
     )(ordered, *counts)
+
+    payload, count_later, base = lax.optimization_barrier((payload, count, base))
+    slots = pl.pallas_call(
+        functools.partial(slot_kernel, blocks),
+        out_shape=jax.ShapeDtypeStruct((2, lanes), jnp.int32),
+        in_specs=[VMEM] * 2,
+        out_specs=VMEM,
+        compiler_params=small,
+        cost_estimate=pl.CostEstimate(
+            flops=1000 * lanes * lanes, bytes_accessed=8 * lanes, transcendentals=0
+        ),
+        name="slots",
+    )(count_later, base)
     got = lax.all_to_all(payload, "seq", split_axis=0, concat_axis=0, tiled=True)
-
-    mask = keep_mask.reshape(sequences, blocks)
-    number = jnp.arange(blocks)
-    rank = jnp.sum(jnp.where(number[None, :] < number[:, None], mask[:, None, :], 0), axis=2)
-    held = jnp.sum(mask, axis=1)
-    wanted = jnp.minimum(number[None, :], held[:, None] - 1)
-    found = (rank[:, None, :] == wanted[:, :, None]) & (mask[:, None, :] > 0)
-    slots = jnp.sum(jnp.where(found, number[None, None, :], 0), axis=2).reshape(lanes)
     table = turn_table(jnp.arange(owners * blocks) * block, width)
     step_table = turn_table(jnp.arange(steps), width)
     sizes = (owners, blocks, block, groups, steps, width, heads, min(4, blocks) * block)
     partial, own_turn = attend(
-        sizes, owner_sequence, slots, held, base, table, step_table, got, prompt_keys, prompt_values
+        sizes, owner_sequence, slots, base, table, step_table, got, prompt_keys, prompt_values
     )
     back = lax.all_to_all(partial, "seq", split_axis=0, concat_axis=0, tiled=True)
     fresh, notes = pl.pallas_call(

time: 46.8 us -> 44.5 us (0.951)
  other arithmetic: 3.53 us -> 0.65 us
  waiting for transfers between devices: 17.7 us -> 18.6 us
    reduce_sum x3 -> x0, other arithmetic: 2.1 us -> none  [the longest x1 0.92 us: shards(): held = jnp.sum(mask, axis=1)]
    ppermute x3, waiting for transfers between devices: 0.01 us -> 2.01 us  [shards(): lax.ppermute(count, 'tp', [(i, i ^ k) for i in range(heads)])]
    all_to_all x1, waiting for transfers between devices: 8.95 us -> 8.22 us  [shards(): lax.all_to_all(payload, 'seq', split_axis=0, concat_axis=0, tiled=True)]
    gt x1 -> x0, other arithmetic: 0.7 us -> none  [shards(): found = (rank[:, None, :] == wanted[:, :, None]) & (mask[:, None, :] > 0)]
  transfers between devices with their start and end apart: 5 -> 5, of which waited for: 2 -> 3; matrix products, arithmetic and copies ran while one was open for 8% -> 1% of each run, Pallas kernels for 1% -> 1%
where the time goes in v4:
time: 44.5 us; the launch traced here: 44.1 us
  waiting for transfers between devices  18.6 us (42%)
  starting transfers between devices  12.6 us (28%)
  Pallas kernels  10.7 us (24%)
  local copies, waits for them, and re-layouts  1.46 us (3%)
  other arithmetic  0.65 us (1%)
    all_to_all x1, waiting for transfers between devices, shards(): lax.all_to_all(partial, 'seq', split_axis=0, concat_axis=0, tiled=True)  8.41 us
    all_to_all x1, waiting for transfers between devices, shards(): lax.all_to_all(payload, 'seq', split_axis=0, concat_axis=0, tiled=True)  8.22 us
    pallas_call x1, Pallas kernels, attend(): pl.pallas_call(functools.partial(attend_kernel, sizes, **kw), out_shape=(...  8.16 us
    all_to_all x1, starting transfers between devices, shards(): lax.all_to_all(payload, 'seq', split_axis=0, concat_axis=0, tiled=True)  5.81 us
    all_to_all x1, starting transfers between devices, shards(): lax.all_to_all(partial, 'seq', split_axis=0, concat_axis=0, tiled=True)  3.64 us
    ppermute x3, starting transfers between devices, shards(): lax.ppermute(count, 'tp', [(i, i ^ k) for i in range(heads)])  3.11 us
    ppermute x3, waiting for transfers between devices, shards(): lax.ppermute(count, 'tp', [(i, i ^ k) for i in range(heads)])  2.01 us
    unnamed x10, local copies, waits for them, and re-layouts  1.46 us
  transfers between devices with their start and end apart: 5, of which 3 were waited for; matrix products, arithmetic and copies ran while one was open for 1% of the time, Pallas kernels for 1%

profile of v4, /device:TPU:0, one launch (start us, length us, event | category | flops | bytes accessed | tf_op | source)
XLA Modules:
  0.0 44.1 jit_solution(9482913098013549737)
XLA Ops:
  0.0 0.7 %copy-done.4 = s32[8,16,1]{1,2,0:T(1,128)S(1)} copy-done((s32[8,16,1]{1,2,0:T(1,128)S(1)}, s32[8,16,1]{1,2,0:T(1,128)}, u32[]{:S(2)}) %copy-start.4) | copy-done | bytes 536
  0.7 0.2 count.1
  0.9 2.4 %collective-permute-start.2 = (f32[8,128]{1,0:T(8,128)S(1)}, f32[8,128]{1,0:T(8,128)S(1)}, u32[]{:S(2)}, u32[]{:S(2)}) collective-permute-start(f32[8,128]{1,0:T(8,128)S(1)} %get-tuple-element.16.refs_0_.count_ref), channel_id=1, source_target_pairs={{0,3},{1,2},{2,1},{3,0},{4,7},{5,6},{6,5},{7,4},{8,11},{9,10},{10,... | collective-permute-start | bytes 12296 | tf_op jit(solution)/shard_map/ppermute | solution.py:392
  3.4 0.6 %collective-permute-start.1 = (f32[8,128]{1,0:T(8,128)S(1)}, f32[8,128]{1,0:T(8,128)S(1)}, u32[]{:S(2)}, u32[]{:S(2)}) collective-permute-start(f32[8,128]{1,0:T(8,128)S(1)} %get-tuple-element.16.refs_0_.count_ref), channel_id=1, source_target_pairs={{0,2},{1,3},{2,0},{3,1},{4,6},{5,7},{6,4},{7,5},{8,10},{9,11},{10,... | collective-permute-start | bytes 12296 | tf_op jit(solution)/shard_map/ppermute | solution.py:392
  3.9 0.1 collective-permute-start
  4.1 0.1 multiply_cosine_fusion.1
  4.2 0.0 copy-start
  4.2 0.7 %copy-done = bf16[1,16,1,1024]{3,1,2,0:T(8,128)(2,1)S(1)} copy-done((bf16[1,16,1,1024]{3,1,2,0:T(8,128)(2,1)S(1)}, bf16[1,16,1,1024]{3,1,2,0:T(8,128)(2,1)}, u32[]{:S(2)}) %copy-start) | copy-done | bytes 32792
  5.0 2.0 %collective-permute-done.1.refs_2_ = f32[8,128]{1,0:T(8,128)S(1)} collective-permute-done((f32[8,128]{1,0:T(8,128)S(1)}, f32[8,128]{1,0:T(8,128)S(1)}, u32[]{:S(2)}, u32[]{:S(2)}) %collective-permute-start.1) | collective-permute-done | bytes 4128 | tf_op jit(solution)/shard_map/ppermute | solution.py:392
  7.0 0.7 %pack.1 = bf16[8,136,128]{2,1,0:T(8,128)(2,1)} custom-call(bf16[128,128]{1,0:T(8,128)(2,1)S(1)} %order.1.query_ref, f32[8,128]{1,0:T(8,128)S(1)} %get-tuple-element.16.refs_0_.count_ref, f32[8,128]{1,0:T(8,128)S(1)} %collective-permute-done.refs_1_, f32[8,128]{1,0:T(8,128)S(1)} %collective-permute-done.1.refs_2_, f32[8,128]{1,0:T(8,128)S(1)} %collective-permute-done.2.refs_3_), custom_call_target="tpu_custom_call" | custom-call | tf_op jit(solution)/shard_map/pack/pallas_call | solution.py:405
  7.7 5.8 %all-to-all-start = ((bf16[8,136,128]{2,1,0:T(8,128)(2,1)}), bf16[8,136,128]{2,1,0:T(8,128)(2,1)S(1)}, u32[]{:S(2)}, u32[]{:S(2)}) async-start(bf16[8,136,128]{2,1,0:T(8,128)(2,1)} %pack.1), calls=%async_computation | async-start | bytes 557056 | tf_op jit(solution)/shard_map/all_to_all | solution.py:426
  13.5 0.1 pad_maximum_fusion.1.step_ref
  13.6 0.3 multiply_cosine_fusion
  13.9 0.1 pad_maximum_fusion.table_ref
  14.0 0.1 slots.1.slot_ref
  14.2 0.0 copy-start.1
  14.2 0.0 copy-start.2
  14.2 0.0 copy-start.3
  14.2 8.2 %all-to-all-done.got_ref = bf16[8,136,128]{2,1,0:T(8,128)(2,1)S(1)} async-done(((bf16[8,136,128]{2,1,0:T(8,128)(2,1)}), bf16[8,136,128]{2,1,0:T(8,128)(2,1)S(1)}, u32[]{:S(2)}, u32[]{:S(2)}) %all-to-all-start) | async-done | bytes 278560 | tf_op jit(solution)/shard_map/all_to_all | solution.py:426
  22.4 8.2 %attend.1 = (bf16[8,136,128]{2,1,0:T(8,128)(2,1)}, f32[16,256]{1,0:T(8,128)S(1)}) custom-call(s32[8]{0:T(128)} %owner_hbm.1, s32[2,128]{1,0:T(2,128)S(1)} %slots.1.slot_ref, f32[8,128]{1,0:T(8,128)S(1)} %get-tuple-element.17.base_ref, f32[128,256]{1,0:T(8,128)S(1)} %pad_maximum_fusion.table_ref, f32[16,256]{1,0:T(8,128)S(1)} %pad_maximum_fusion.1.step_ref, ...), custom_call_target="tpu_custom_call" | custom-call | tf_op jit(solution)/shard_map/attend/pallas_call | solution.py:327
  30.6 3.6 %all-to-all-start.1 = ((bf16[8,136,128]{2,1,0:T(8,128)(2,1)}), bf16[8,136,128]{2,1,0:T(8,128)(2,1)S(1)}, u32[]{:S(2)}, u32[]{:S(2)}) async-start(bf16[8,136,128]{2,1,0:T(8,128)(2,1)} %get-tuple-element.19), calls=%async_computation.1 | async-start | bytes 557056 | tf_op jit(solution)/shard_map/all_to_all | solution.py:433
  34.3 0.4 fresh.1
  34.7 8.4 %all-to-all-done.1.got_ref = bf16[8,136,128]{2,1,0:T(8,128)(2,1)S(1)} async-done(((bf16[8,136,128]{2,1,0:T(8,128)(2,1)}), bf16[8,136,128]{2,1,0:T(8,128)(2,1)S(1)}, u32[]{:S(2)}, u32[]{:S(2)}) %all-to-all-start.1) | async-done | bytes 278560 | tf_op jit(solution)/shard_map/all_to_all | solution.py:433
  43.1 1.0 %merge.1 = bf16[16,1024]{1,0:T(8,128)(2,1)} custom-call(bf16[8,136,128]{2,1,0:T(8,128)(2,1)S(1)} %all-to-all-done.1.got_ref, f32[128,128]{1,0:T(8,128)S(1)} %get-tuple-element.21.fresh_ref, f32[8,128]{1,0:T(8,128)S(1)} %get-tuple-element.22.note_ref), custom_call_target="tpu_custom_call" | custom-call | tf_op jit(solution)/shard_map/merge/pallas_call | solution.py:448
  (10 shorter events, 0.0 us)
Async XLA Ops:
  0.0 0.7 %copy-start.4 = (s32[8,16,1]{1,2,0:T(1,128)S(1)}, s32[8,16,1]{1,2,0:T(1,128)}, u32[]{:S(2)}) copy-start(s32[8,16,1]{1,2,0:T(1,128)} %param.9) | copy-start | bytes 1540
  0.9 4.0 %collective-permute-start.2 = (f32[8,128]{1,0:T(8,128)S(1)}, f32[8,128]{1,0:T(8,128)S(1)}, u32[]{:S(2)}, u32[]{:S(2)}) collective-permute-start(f32[8,128]{1,0:T(8,128)S(1)} %get-tuple-element.16.refs_0_.count_ref), channel_id=1, source_target_pairs={{0,3},{1,2},{2,1},{3,0},{4,7},{5,6},{6,5},{7,4},{8,11},{9,10},{10,... | collective-permute-start | bytes 12296 | tf_op jit(solution)/shard_map/ppermute | solution.py:392
  3.4 3.6 %collective-permute-start.1 = (f32[8,128]{1,0:T(8,128)S(1)}, f32[8,128]{1,0:T(8,128)S(1)}, u32[]{:S(2)}, u32[]{:S(2)}) collective-permute-start(f32[8,128]{1,0:T(8,128)S(1)} %get-tuple-element.16.refs_0_.count_ref), channel_id=1, source_target_pairs={{0,2},{1,3},{2,0},{3,1},{4,6},{5,7},{6,4},{7,5},{8,10},{9,11},{10,... | collective-permute-start | bytes 12296 | tf_op jit(solution)/shard_map/ppermute | solution.py:392
  3.9 3.0 %collective-permute-start = (f32[8,128]{1,0:T(8,128)S(1)}, f32[8,128]{1,0:T(8,128)S(1)}, u32[]{:S(2)}, u32[]{:S(2)}) collective-permute-start(f32[8,128]{1,0:T(8,128)S(1)} %get-tuple-element.16.refs_0_.count_ref), channel_id=1, source_target_pairs={{0,1},{1,0},{2,3},{3,2},{4,5},{5,4},{6,7},{7,6},{8,9},{9,8},{10,11... | collective-permute-start | bytes 12296 | tf_op jit(solution)/shard_map/ppermute | solution.py:392
  4.2 0.8 %copy-start = (bf16[1,16,1,1024]{3,1,2,0:T(8,128)(2,1)S(1)}, bf16[1,16,1,1024]{3,1,2,0:T(8,128)(2,1)}, u32[]{:S(2)}) copy-start(bf16[1,16,1,1024]{3,1,2,0:T(8,128)(2,1)} %param.11) | copy-start | bytes 98308
  7.7 14.7 %all-to-all-start = ((bf16[8,136,128]{2,1,0:T(8,128)(2,1)}), bf16[8,136,128]{2,1,0:T(8,128)(2,1)S(1)}, u32[]{:S(2)}, u32[]{:S(2)}) async-start(bf16[8,136,128]{2,1,0:T(8,128)(2,1)} %pack.1), calls=%async_computation | async-start | bytes 557056 | tf_op jit(solution)/shard_map/all_to_all | solution.py:426
  14.2 20.1 %copy-start.1 = (bf16[1,16,1,1024]{3,1,2,0:T(8,128)(2,1)S(1)}, bf16[1,16,1,1024]{3,1,2,0:T(8,128)(2,1)}, u32[]{:S(2)}) copy-start(bf16[1,16,1,1024]{3,1,2,0:T(8,128)(2,1)} %param.11) | copy-start | bytes 98308
  14.2 20.1 %copy-start.2 = (bf16[1,16,128]{2,1,0:T(8,128)(2,1)S(1)}, bf16[1,16,128]{2,1,0:T(8,128)(2,1)}, u32[]{:S(2)}) copy-start(bf16[1,16,128]{2,1,0:T(8,128)(2,1)} %param.12) | copy-start | bytes 12292
  14.2 20.1 %copy-start.3 = (bf16[1,16,128]{2,1,0:T(8,128)(2,1)S(1)}, bf16[1,16,128]{2,1,0:T(8,128)(2,1)}, u32[]{:S(2)}) copy-start(bf16[1,16,128]{2,1,0:T(8,128)(2,1)} %param.13) | copy-start | bytes 12292
  30.6 12.5 %all-to-all-start.1 = ((bf16[8,136,128]{2,1,0:T(8,128)(2,1)}), bf16[8,136,128]{2,1,0:T(8,128)(2,1)S(1)}, u32[]{:S(2)}, u32[]{:S(2)}) async-start(bf16[8,136,128]{2,1,0:T(8,128)(2,1)} %get-tuple-element.19), calls=%async_computation.1 | async-start | bytes 557056 | tf_op jit(solution)/shard_map/all_to_all | solution.py:433

commit v5 on v4

--- a/solution.py
+++ b/solution.py
@@ -74,50 +74,95 @@
     out_ref[1:2, :] = held.astype(jnp.int32)
 
 
-def pack_kernel(query_ref, *refs):
-    out_ref = refs[-1]
-    rows = query_ref.shape[0]
-    query = query_ref[...]
-    counts = [ref[0:1, :] for ref in refs[:-1]]
-    fill = refs[0][len(counts) : EXTRA, :]
-    counts = jnp.concatenate(counts + [fill], axis=0).astype(BF)
+def pack_kernel(groups, width, query_ref, count_ref, out_ref):
+    steps = query_ref.shape[0]
+    rows = groups * steps
+    parts = [query_ref[:, g * width : (g + 1) * width] for g in range(groups)]
+    counts = count_ref[...].astype(BF)
     for target in range(out_ref.shape[0]):
-        out_ref[target, 0:rows, :] = query
+        for g in range(groups):
+            out_ref[target, g * steps : (g + 1) * steps, :] = parts[g]
         out_ref[target, rows : rows + EXTRA, :] = counts
 
 
-def order_kernel(groups, width, query_ref, out_ref):
-    steps = query_ref.shape[0]
-    for g in range(groups):
-        out_ref[g * steps : (g + 1) * steps, :] = query_ref[:, g * width : (g + 1) * width]
+def total_kernel(rows, got_ref, out_ref):
+    total = jnp.zeros(out_ref.shape, F32)
+    for i in range(got_ref.shape[0]):
+        total = total + got_ref[i, rows : rows + EXTRA, :].astype(F32)
+    out_ref[...] = total
+
+
+def look_up(pick, table_ref, cos_to, sin_to):
+    table = table_ref[...]
+    pick = pick.astype(F32).T.astype(BF)
+    parts = []
+    for _ in range(3):
+        part = table.astype(BF)
+        parts.append(part)
+        table = table - part.astype(F32)
+    found = sum(jnp.dot(pick, part, preferred_element_type=F32) for part in parts[::-1])
+    width = cos_to.shape[1]
+    cos_to[...] = found[:, 0:width]
+    sin_to[...] = found[:, width:]
+
+
+def turn_kernel(sizes, slot_ref, base_ref, table_ref, got_ref, key_hbm, out_ref, cos_k, sin_k, key_ref, key_sem):
+    owners, blocks, block, groups, steps, width, heads, chunk = sizes
+    rows = groups * steps
+    lanes = owners * blocks
+    me = lax.axis_index("seq")
+
+    def fetch(s):
+        return pltpu.make_async_copy(key_hbm.at[s], key_ref.at[s], key_sem.at[s])
+
+    @pl.loop(0, owners)
+    def _(s):
+        fetch(s).start()
+
+    before = jnp.zeros((1, lanes), F32)
+    for i in range(owners):
+        piece = got_ref[i, rows : rows + EXTRA, :].astype(F32)
+        before = before + jnp.where(i < me, piece[0:1], 0.0)
+    dropped = base_ref[0:1, :] - before
+    entry = iota((table_ref.shape[0], lanes), 0).astype(F32)
+    look_up(entry == dropped, table_ref, cos_k, sin_k)
+
+    @pl.loop(0, owners)
+    def _(s):
+        fetch(s).wait()
+        for r in range(blocks):
+            b = slot_ref[0, s * blocks + r]
+            cosine = cos_k[pl.ds(s * blocks + b, 1), :]
+            sine = sin_k[pl.ds(s * blocks + b, 1), :]
+            x = key_ref[s, pl.ds(pl.multiple_of(b * block, block), block), :].astype(F32)
+            out_ref[s, r * block : (r + 1) * block, :] = turned(x, cosine, -sine).astype(BF)
 
 
 def attend_kernel(
     sizes,
     owner_hbm,
     slot_ref,
-    base_ref,
+    total_ref,
+    other_ref,
+    another_ref,
+    last_ref,
     table_ref,
     step_ref,
     got_ref,
-    key_hbm,
+    turned_ref,
     value_hbm,
     out_ref,
     own_ref,
-    cos_k,
-    sin_k,
     cos_q,
     sin_q,
     score_a,
     score_b,
     best_a,
     best_b,
-    key_ref,
     value_ref,
     owner_ref,
     place_ref,
     owner_sem,
-    key_sem,
     value_sem,
 ):
     owners, blocks, block, groups, steps, width, heads, chunk = sizes
@@ -128,39 +173,17 @@
     fetch_owner.start()
 
     def fetch(s):
-        return (
-            pltpu.make_async_copy(key_hbm.at[s], key_ref.at[s], key_sem.at[s]),
-            pltpu.make_async_copy(value_hbm.at[s], value_ref.at[s], value_sem.at[s]),
-        )
+        return pltpu.make_async_copy(value_hbm.at[s], value_ref.at[s], value_sem.at[s])
 
     @pl.loop(0, owners)
     def _(s):
-        for copy in fetch(s):
-            copy.start()
-
-    before = jnp.zeros((1, lanes), F32)
-    total = jnp.zeros((heads, lanes), F32)
-    for i in range(owners):
-        piece = got_ref[i, rows : rows + EXTRA, :].astype(F32)
-        total = total + piece[0:heads]
-        before = before + jnp.where(i < me, piece[0:1], 0.0)
-    longest = jnp.max(total, axis=0, keepdims=True)
-    dropped = base_ref[0:1, :] - before
-    entry = lax.broadcasted_iota(jnp.int32, (table_ref.shape[0], lanes), 0).astype(F32)
-    pick_k = (entry == dropped).astype(F32)
-    pick_q = (entry == longest).astype(F32)
-    dims = (((0,), (0,)), ((), ()))
-    table = table_ref[...]
-    parts = []
-    for _ in range(3):
-        part = table.astype(BF)
-        parts.append(part)
-        table = table - part.astype(F32)
-    for pick, cos_to, sin_to in ((pick_k, cos_k, sin_k), (pick_q, cos_q, sin_q)):
-        pick = pick.T.astype(BF)
-        found = sum(jnp.dot(pick, part, preferred_element_type=F32) for part in parts[::-1])
-        cos_to[...] = found[:, 0:width]
-        sin_to[...] = found[:, width:]
+        fetch(s).start()
+
+    longest = total_ref[0:1, :]
+    for ref in (other_ref, another_ref, last_ref):
+        longest = jnp.maximum(longest, ref[0:1, :])
+    entry = iota((table_ref.shape[0], lanes), 0).astype(F32)
+    look_up(entry == longest, table_ref, cos_q, sin_q)
     fetch_owner.wait()
     step_cos, step_sin = step_ref[:, 0:width], step_ref[:, width:]
     factor = math.log2(math.e) / math.sqrt(width)
@@ -198,16 +221,9 @@
             slots = range(c * per, (c + 1) * per)
             if ahead is not None:
                 scores_out, best_out = fill
-                keys = []
-                for r in slots:
-                    b = slot_ref[0, ahead * blocks + r]
-                    cosine = cos_k[pl.ds(ahead * blocks + b, 1), :]
-                    sine = sin_k[pl.ds(ahead * blocks + b, 1), :]
-                    x = key_ref[ahead, pl.ds(pl.multiple_of(b * block, block), block), :]
-                    keys.append(turned(x.astype(F32), cosine, -sine).astype(BF))
                 scores = lax.dot_general(
                     query,
-                    jnp.concatenate(keys, axis=0),
+                    turned_ref[ahead, c * chunk : (c + 1) * chunk, :],
                     (((1,), (1,)), ((), ())),
                     preferred_element_type=F32,
                 )
@@ -240,21 +256,17 @@
             out_ref[o, rows : rows + EXTRA, :] = notes.T[0:EXTRA].astype(BF)
 
     even, odd = (score_a, best_a), (score_b, best_b)
-    fetch(0)[0].wait()
     step_over(0, even, None, None)
 
     @pl.loop(0, owners // 2 - 1)
     def _(i):
-        fetch(2 * i + 1)[0].wait()
-        fetch(2 * i + 2)[0].wait()
-        fetch(2 * i)[1].wait()
-        fetch(2 * i + 1)[1].wait()
+        fetch(2 * i).wait()
+        fetch(2 * i + 1).wait()
         step_over(2 * i + 1, odd, 2 * i, even)
         step_over(2 * i + 2, even, 2 * i + 1, odd)
 
-    fetch(owners - 1)[0].wait()
-    fetch(owners - 2)[1].wait()
-    fetch(owners - 1)[1].wait()
+    fetch(owners - 2).wait()
+    fetch(owners - 1).wait()
     step_over(owners - 1, odd, owners - 2, even)
     step_over(None, None, owners - 1, odd)
 
@@ -321,44 +333,62 @@
 SMEM = pl.BlockSpec(memory_space=pltpu.SMEM)
 
 
-def attend(sizes, owner, slots, base, table, step_table, got, keys, values, **kw):
+def turn(sizes, slots, base, table, got, keys):
+    owners, blocks, block, groups, steps, width, heads, chunk = sizes
+    lanes = owners * blocks
+    return pl.pallas_call(
+        functools.partial(turn_kernel, sizes),
+        out_shape=jax.ShapeDtypeStruct(keys.shape, BF),
+        in_specs=[SMEM] + [VMEM] * 3 + [ANY],
+        out_specs=VMEM,
+        scratch_shapes=[
+            pltpu.VMEM((lanes, width), F32),
+            pltpu.VMEM((lanes, width), F32),
+            pltpu.VMEM(keys.shape, BF),
+            pltpu.SemaphoreType.DMA((owners,)),
+        ],
+        compiler_params=pltpu.CompilerParams(vmem_limit_bytes=12 * 1024 * 1024),
+        cost_estimate=pl.CostEstimate(
+            flops=256 * keys.size, bytes_accessed=4 * keys.size, transcendentals=0
+        ),
+        name="turn",
+    )(slots, base, table, got, pltpu.with_memory_space_constraint(keys, pltpu.HBM))
+
+
+def attend(sizes, owner, slots, totals, table, step_table, got, keys, values):
     owners, blocks, block, groups, steps, width, heads, chunk = sizes
     rows, lanes = groups * steps, owners * blocks
     return pl.pallas_call(
-        functools.partial(attend_kernel, sizes, **kw),
+        functools.partial(attend_kernel, sizes),
         out_shape=(
             jax.ShapeDtypeStruct((owners, rows + EXTRA, width), BF),
             jax.ShapeDtypeStruct((steps, 2 * width), F32),
         ),
-        in_specs=[ANY] + [SMEM] + [VMEM] * 4 + [ANY] * 2,
+        in_specs=[ANY] + [SMEM] + [VMEM] * 8 + [ANY],
         out_specs=(VMEM, VMEM),
         scratch_shapes=[
-            pltpu.VMEM((lanes, width), F32),
-            pltpu.VMEM((lanes, width), F32),
             pltpu.VMEM((lanes, width), F32),
             pltpu.VMEM((lanes, width), F32),
             pltpu.VMEM((rows, blocks * block), F32),
             pltpu.VMEM((rows, blocks * block), F32),
             pltpu.VMEM((rows, block), F32),
             pltpu.VMEM((rows, block), F32),
-            pltpu.VMEM(keys.shape, BF),
             pltpu.VMEM(values.shape, BF),
             pltpu.SMEM((owners,), jnp.int32),
             pltpu.SMEM((owners,), jnp.int32),
             pltpu.SemaphoreType.DMA,
             pltpu.SemaphoreType.DMA((owners,)),
-            pltpu.SemaphoreType.DMA((owners,)),
         ],
-        compiler_params=pltpu.CompilerParams(vmem_limit_bytes=24 * 1024 * 1024),
+        compiler_params=pltpu.CompilerParams(vmem_limit_bytes=16 * 1024 * 1024),
         name="attend",
     )(
         pltpu.with_memory_space_constraint(owner, pltpu.HBM),
         slots,
-        base,
+        *totals,
         table,
         step_table,
         got,
-        pltpu.with_memory_space_constraint(keys, pltpu.HBM),
+        keys,
         pltpu.with_memory_space_constraint(values, pltpu.HBM),
     )
 
@@ -388,29 +418,14 @@
         compiler_params=small,
         name="count",
     )(keep_mask.transpose(0, 2, 1))
-    counts = [count] + [
-        lax.ppermute(count, "tp", [(i, i ^ k) for i in range(heads)]) for k in range(1, heads)
-    ]
-    ordered = pl.pallas_call(
-        functools.partial(order_kernel, groups, width),
-        out_shape=jax.ShapeDtypeStruct((rows, width), BF),
-        in_specs=[VMEM],
+    payload = pl.pallas_call(
+        functools.partial(pack_kernel, groups, width),
+        out_shape=jax.ShapeDtypeStruct((owners, rows + EXTRA, width), BF),
+        in_specs=[VMEM] * 2,
         out_specs=VMEM,
         compiler_params=small,
-        cost_estimate=pl.CostEstimate(
-            flops=rows * width, bytes_accessed=4 * rows * width, transcendentals=0
-        ),
-        name="order",
-    )(query)
-    payload = pl.pallas_call(
-        pack_kernel,
-        out_shape=jax.ShapeDtypeStruct((owners, rows + EXTRA, width), BF),
-        in_specs=[VMEM] * (1 + heads),
-        out_specs=VMEM,
-        compiler_params=small,
         name="pack",
-    )(ordered, *counts)
-
+    )(query, count)
     payload, count_later, base = lax.optimization_barrier((payload, count, base))
     slots = pl.pallas_call(
         functools.partial(slot_kernel, blocks),
@@ -424,11 +439,24 @@
         name="slots",
     )(count_later, base)
     got = lax.all_to_all(payload, "seq", split_axis=0, concat_axis=0, tiled=True)
+
     table = turn_table(jnp.arange(owners * blocks) * block, width)
     step_table = turn_table(jnp.arange(steps), width)
     sizes = (owners, blocks, block, groups, steps, width, heads, min(4, blocks) * block)
+    total = pl.pallas_call(
+        functools.partial(total_kernel, rows),
+        out_shape=jax.ShapeDtypeStruct((EXTRA, lanes), F32),
+        in_specs=[VMEM],
+        out_specs=VMEM,
+        compiler_params=small,
+        name="total",
+    )(got)
+    totals = [total] + [
+        lax.ppermute(total, "tp", [(i, i ^ k) for i in range(heads)]) for k in range(1, heads)
+    ]
+    keys = turn(sizes, slots, base, table, got, prompt_keys)
     partial, own_turn = attend(
-        sizes, owner_sequence, slots, base, table, step_table, got, prompt_keys, prompt_values
+        sizes, owner_sequence, slots, totals, table, step_table, got, keys, prompt_values
     )
     back = lax.all_to_all(partial, "seq", split_axis=0, concat_axis=0, tiled=True)
     fresh, notes = pl.pallas_call(

time: 44.5 us -> 45.7 us (1.027)
  Pallas kernels: 10.7 us -> 12.7 us
  waiting for transfers between devices: 18.6 us -> 17.7 us
    ppermute x3, waiting for transfers between devices: 2.01 us -> 0.01 us  [shards(): lax.ppermute(total, 'tp', [(i, i ^ k) for i in range(heads)])]
    pallas_call x3 -> x4, Pallas kernels: 8.9 us -> 10.9 us  [the longest x1 6.58 us: attend(): pl.pallas_call(functools.partial(attend_kernel, sizes), out_shape=(jax.Sh...]
    all_to_all x1, starting transfers between devices: 5.81 us -> 7.28 us  [shards(): lax.all_to_all(payload, 'seq', split_axis=0, concat_axis=0, tiled=True)]
    ppermute x3, starting transfers between devices: 3.11 us -> 1.86 us  [shards(): lax.ppermute(total, 'tp', [(i, i ^ k) for i in range(heads)])]
    all_to_all x1, waiting for transfers between devices: 8.41 us -> 9.21 us  [shards(): lax.all_to_all(partial, 'seq', split_axis=0, concat_axis=0, tiled=True)]
  transfers between devices with their start and end apart: 5 -> 5, of which waited for: 3 -> 2; matrix products, arithmetic and copies ran while one was open for 1% -> 1% of each run, Pallas kernels for 1% -> 9%
where the time goes in v5:
time: 45.7 us; the launch traced here: 45.3 us
  waiting for transfers between devices  17.7 us (39%)
  Pallas kernels  12.7 us (28%)
  starting transfers between devices  12.7 us (28%)
  local copies, waits for them, and re-layouts  1.46 us (3%)
  other arithmetic  0.65 us (1%)
    all_to_all x1, waiting for transfers between devices, shards(): lax.all_to_all(partial, 'seq', split_axis=0, concat_axis=0, tiled=True)  9.21 us
    all_to_all x1, waiting for transfers between devices, shards(): lax.all_to_all(payload, 'seq', split_axis=0, concat_axis=0, tiled=True)  8.46 us
    all_to_all x1, starting transfers between devices, shards(): lax.all_to_all(payload, 'seq', split_axis=0, concat_axis=0, tiled=True)  7.28 us
    pallas_call x1, Pallas kernels, attend(): pl.pallas_call(functools.partial(attend_kernel, sizes), out_shape=(jax.Sh...  6.58 us
    all_to_all x1, starting transfers between devices, shards(): lax.all_to_all(partial, 'seq', split_axis=0, concat_axis=0, tiled=True)  3.6 us
    pallas_call x1, Pallas kernels, turn(): pl.pallas_call(functools.partial(turn_kernel, sizes), out_shape=jax.Shape...  3.57 us
    ppermute x3, starting transfers between devices, shards(): lax.ppermute(total, 'tp', [(i, i ^ k) for i in range(heads)])  1.86 us
    unnamed x10, local copies, waits for them, and re-layouts  1.46 us
  transfers between devices with their start and end apart: 5, of which 2 were waited for; matrix products, arithmetic and copies ran while one was open for 1% of the time, Pallas kernels for 9%

profile of v5, /device:TPU:0, one launch (start us, length us, event | category | flops | bytes accessed | tf_op | source)
XLA Modules:
  0.0 45.3 jit_solution(2584385786472552971)
XLA Ops:
  0.0 0.7 %copy-done.4 = s32[8,16,1]{1,2,0:T(1,128)S(1)} copy-done((s32[8,16,1]{1,2,0:T(1,128)S(1)}, s32[8,16,1]{1,2,0:T(1,128)}, u32[]{:S(2)}) %copy-start.4) | copy-done | bytes 536
  0.7 0.2 count.1
  0.9 0.8 %copy-done = bf16[1,16,1,1024]{3,1,2,0:T(8,128)(2,1)S(1)} copy-done((bf16[1,16,1,1024]{3,1,2,0:T(8,128)(2,1)S(1)}, bf16[1,16,1,1024]{3,1,2,0:T(8,128)(2,1)}, u32[]{:S(2)}) %copy-start) | copy-done | bytes 32792
  1.7 0.7 %pack.1 = bf16[8,136,128]{2,1,0:T(8,128)(2,1)} custom-call(bf16[16,1024]{1,0:T(8,128)(2,1)S(1)} %bitcast.7, f32[8,128]{1,0:T(8,128)S(1)} %get-tuple-element.16.count_ref), custom_call_target="tpu_custom_call" | custom-call | tf_op jit(solution)/shard_map/pack/pallas_call | solution.py:421
  2.4 7.3 %all-to-all-start = ((bf16[8,136,128]{2,1,0:T(8,128)(2,1)}), bf16[8,136,128]{2,1,0:T(8,128)(2,1)S(1)}, u32[]{:S(2)}, u32[]{:S(2)}) async-start(bf16[8,136,128]{2,1,0:T(8,128)(2,1)} %pack.1), calls=%async_computation | async-start | bytes 557056 | tf_op jit(solution)/shard_map/all_to_all | solution.py:441
  9.7 0.1 multiply_cosine_fusion.1
  9.9 0.1 slots.1.slot_ref
  10.0 0.1 pad_maximum_fusion.1.step_ref
  10.1 0.3 multiply_cosine_fusion
  10.4 0.1 pad_maximum_fusion.table_ref
  10.5 8.5 %all-to-all-done.got_ref = bf16[8,136,128]{2,1,0:T(8,128)(2,1)S(1)} async-done(((bf16[8,136,128]{2,1,0:T(8,128)(2,1)}), bf16[8,136,128]{2,1,0:T(8,128)(2,1)S(1)}, u32[]{:S(2)}, u32[]{:S(2)}) %all-to-all-start) | async-done | bytes 278560 | tf_op jit(solution)/shard_map/all_to_all | solution.py:441
  19.0 0.0 collective-permute-start.2
  19.0 1.6 %collective-permute-start.1 = (f32[8,128]{1,0:T(8,128)S(1)}, f32[8,128]{1,0:T(8,128)S(1)}, u32[]{:S(2)}, u32[]{:S(2)}) collective-permute-start(f32[8,128]{1,0:T(8,128)S(1)} %total.1.total_ref), channel_id=1, source_target_pairs={{0,2},{1,3},{2,0},{3,1},{4,6},{5,7},{6,4},{7,5},{8,10},{9,11},{10,... | collective-permute-start | bytes 12296 | tf_op jit(solution)/shard_map/ppermute | solution.py:455
  20.6 0.3 collective-permute-start
  20.8 3.6 %turn.1.turned_ref = bf16[8,2048,128]{2,1,0:T(8,128)(2,1)S(1)} custom-call(s32[2,128]{1,0:T(2,128)S(1)} %slots.1.slot_ref, f32[8,128]{1,0:T(8,128)S(1)} %get-tuple-element.17.base_ref, f32[128,256]{1,0:T(8,128)S(1)} %pad_maximum_fusion.table_ref, bf16[8,136,128]{2,1,0:T(8,128)(2,1)S(1)} %all-to-all-done.got_ref, bf16[8,2048,128]{2,1,0:T(8,128)(2,1)} %key_hbm.1), custom_call_target="tpu_custom_call" | custom-call | flops 536870912 | bytes 8388608 | tf_op jit(solution)/shard_map/turn/pallas_call | solution.py:339
  24.4 0.0 copy-start.1
  24.4 0.0 copy-start.2
  24.4 0.0 copy-start.3
  24.5 0.0 collective-permute-done.1.another_ref
  24.5 6.6 %attend.1 = (bf16[8,136,128]{2,1,0:T(8,128)(2,1)}, f32[16,256]{1,0:T(8,128)S(1)}) custom-call(s32[8]{0:T(128)} %owner_hbm.1, s32[2,128]{1,0:T(2,128)S(1)} %slots.1.slot_ref, f32[8,128]{1,0:T(8,128)S(1)} %total.1.total_ref, f32[8,128]{1,0:T(8,128)S(1)} %collective-permute-done.other_ref, f32[8,128]{1,0:T(8,128)S(1)} %collective-permute-done.1.another_ref, ...), custom_call_target="tpu_custom_call" | custom-call | tf_op jit(solution)/shard_map/attend/pallas_call | solution.py:361
  31.1 3.6 %all-to-all-start.1 = ((bf16[8,136,128]{2,1,0:T(8,128)(2,1)}), bf16[8,136,128]{2,1,0:T(8,128)(2,1)S(1)}, u32[]{:S(2)}, u32[]{:S(2)}) async-start(bf16[8,136,128]{2,1,0:T(8,128)(2,1)} %get-tuple-element.19), calls=%async_computation.1 | async-start | bytes 557056 | tf_op jit(solution)/shard_map/all_to_all | solution.py:461
  34.7 0.4 fresh.1
  35.1 9.2 %all-to-all-done.1.got_ref = bf16[8,136,128]{2,1,0:T(8,128)(2,1)S(1)} async-done(((bf16[8,136,128]{2,1,0:T(8,128)(2,1)}), bf16[8,136,128]{2,1,0:T(8,128)(2,1)S(1)}, u32[]{:S(2)}, u32[]{:S(2)}) %all-to-all-start.1) | async-done | bytes 278560 | tf_op jit(solution)/shard_map/all_to_all | solution.py:461
  44.3 1.0 %merge.1 = bf16[16,1024]{1,0:T(8,128)(2,1)} custom-call(bf16[8,136,128]{2,1,0:T(8,128)(2,1)S(1)} %all-to-all-done.1.got_ref, f32[128,128]{1,0:T(8,128)S(1)} %get-tuple-element.21.fresh_ref, f32[8,128]{1,0:T(8,128)S(1)} %get-tuple-element.22.note_ref), custom_call_target="tpu_custom_call" | custom-call | tf_op jit(solution)/shard_map/merge/pallas_call | solution.py:476
  (11 shorter events, 0.0 us)
Async XLA Ops:
  0.0 0.7 %copy-start.4 = (s32[8,16,1]{1,2,0:T(1,128)S(1)}, s32[8,16,1]{1,2,0:T(1,128)}, u32[]{:S(2)}) copy-start(s32[8,16,1]{1,2,0:T(1,128)} %param.9) | copy-start | bytes 1540
  0.9 0.8 %copy-start = (bf16[1,16,1,1024]{3,1,2,0:T(8,128)(2,1)S(1)}, bf16[1,16,1,1024]{3,1,2,0:T(8,128)(2,1)}, u32[]{:S(2)}) copy-start(bf16[1,16,1,1024]{3,1,2,0:T(8,128)(2,1)} %param.11) | copy-start | bytes 98308
  2.4 16.5 %all-to-all-start = ((bf16[8,136,128]{2,1,0:T(8,128)(2,1)}), bf16[8,136,128]{2,1,0:T(8,128)(2,1)S(1)}, u32[]{:S(2)}, u32[]{:S(2)}) async-start(bf16[8,136,128]{2,1,0:T(8,128)(2,1)} %pack.1), calls=%async_computation | async-start | bytes 557056 | tf_op jit(solution)/shard_map/all_to_all | solution.py:441
  19.0 5.5 %collective-permute-start.2 = (f32[8,128]{1,0:T(8,128)S(1)}, f32[8,128]{1,0:T(8,128)S(1)}, u32[]{:S(2)}, u32[]{:S(2)}) collective-permute-start(f32[8,128]{1,0:T(8,128)S(1)} %total.1.total_ref), channel_id=1, source_target_pairs={{0,3},{1,2},{2,1},{3,0},{4,7},{5,6},{6,5},{7,4},{8,11},{9,10},{10,... | collective-permute-start | bytes 12296 | tf_op jit(solution)/shard_map/ppermute | solution.py:455
  19.0 5.5 %collective-permute-start.1 = (f32[8,128]{1,0:T(8,128)S(1)}, f32[8,128]{1,0:T(8,128)S(1)}, u32[]{:S(2)}, u32[]{:S(2)}) collective-permute-start(f32[8,128]{1,0:T(8,128)S(1)} %total.1.total_ref), channel_id=1, source_target_pairs={{0,2},{1,3},{2,0},{3,1},{4,6},{5,7},{6,4},{7,5},{8,10},{9,11},{10,... | collective-permute-start | bytes 12296 | tf_op jit(solution)/shard_map/ppermute | solution.py:455
  20.6 3.9 %collective-permute-start = (f32[8,128]{1,0:T(8,128)S(1)}, f32[8,128]{1,0:T(8,128)S(1)}, u32[]{:S(2)}, u32[]{:S(2)}) collective-permute-start(f32[8,128]{1,0:T(8,128)S(1)} %total.1.total_ref), channel_id=1, source_target_pairs={{0,1},{1,0},{2,3},{3,2},{4,5},{5,4},{6,7},{7,6},{8,9},{9,8},{10,11... | collective-permute-start | bytes 12296 | tf_op jit(solution)/shard_map/ppermute | solution.py:455
  24.4 10.3 %copy-start.1 = (bf16[1,16,1,1024]{3,1,2,0:T(8,128)(2,1)S(1)}, bf16[1,16,1,1024]{3,1,2,0:T(8,128)(2,1)}, u32[]{:S(2)}) copy-start(bf16[1,16,1,1024]{3,1,2,0:T(8,128)(2,1)} %param.11) | copy-start | bytes 98308
  24.4 10.3 %copy-start.2 = (bf16[1,16,128]{2,1,0:T(8,128)(2,1)S(1)}, bf16[1,16,128]{2,1,0:T(8,128)(2,1)}, u32[]{:S(2)}) copy-start(bf16[1,16,128]{2,1,0:T(8,128)(2,1)} %param.12) | copy-start | bytes 12292
  24.4 10.3 %copy-start.3 = (bf16[1,16,128]{2,1,0:T(8,128)(2,1)S(1)}, bf16[1,16,128]{2,1,0:T(8,128)(2,1)}, u32[]{:S(2)}) copy-start(bf16[1,16,128]{2,1,0:T(8,128)(2,1)} %param.13) | copy-start | bytes 12292
  31.1 13.3 %all-to-all-start.1 = ((bf16[8,136,128]{2,1,0:T(8,128)(2,1)}), bf16[8,136,128]{2,1,0:T(8,128)(2,1)S(1)}, u32[]{:S(2)}, u32[]{:S(2)}) async-start(bf16[8,136,128]{2,1,0:T(8,128)(2,1)} %get-tuple-element.19), calls=%async_computation.1 | async-start | bytes 557056 | tf_op jit(solution)/shard_map/all_to_all | solution.py:461
